TPU v7x, 32 devices: a whole 2x2x4 slice. The times are simulated.
32 devices in a mesh: dp: 16 (over z, x, core), tensor: 2 (over y).
Axes of the slice: x: 2, y: 2, z: 4, core: 2. Of those that a mesh axis runs over, the one named last changes fastest.
Arguments:
- block_input: bfloat16 [32, 577, 1024], P('dp'), may hold values from -6 to 6
- first_scale: float32 [1024], replicated, may hold values from 0.5 to 1.5
- first_shift: float32 [1024], replicated, may hold values from -3 to 3
- heads_weight: bfloat16 [1024, 3, 1024], P(None, None, 'tensor'), may hold values from -0.1875 to 0.1875
- heads_bias: float32 [2, 1024], P(None, 'tensor'), may hold values from -3 to 3
- mixing_weight: bfloat16 [1024, 1024], P('tensor'), may hold values from -0.75 to 0.75
- mixing_bias: float32 [1024], replicated, may hold values from -3 to 3
- second_scale: float32 [1024], replicated, may hold values from 0.5 to 1.5
- second_shift: float32 [1024], replicated, may hold values from -3 to 3
- expand_weight: bfloat16 [1024, 4096], P(None, 'tensor'), may hold values from -0.1875 to 0.1875
- expand_bias: float32 [4096], P('tensor'), may hold values from -3 to 3
- shrink_weight: bfloat16 [4096, 1024], P('tensor'), may hold values from -0.09375 to 0.09375
- shrink_bias: float32 [1024], replicated, may hold values from -3 to 3
- output_grad: bfloat16 [32, 577, 1024], P('dp'), may hold values from -6 to 6
Outputs:
- block_output: bfloat16 [32, 577, 1024], P('dp')
- input_grad: bfloat16 [32, 577, 1024], P('dp')
- heads_weight_grad: float32 [1024, 3, 1024], P(None, None, 'tensor')
- heads_bias_grad: float32 [2, 1024], P(None, 'tensor')
- mixing_weight_grad: float32 [1024, 1024], P('tensor')
- mixing_bias_grad: float32 [1024], replicated
- second_scale_grad: float32 [1024], replicated
- second_shift_grad: float32 [1024], replicated
- expand_weight_grad: float32 [1024, 4096], P(None, 'tensor')
- expand_bias_grad: float32 [4096], P('tensor')
- shrink_weight_grad: float32 [4096, 1024], P('tensor')
- shrink_bias_grad: float32 [1024], replicated
- first_scale_grad: float32 [1024], replicated
- first_shift_grad: float32 [1024], replicated
All inputs are finite; a program needn't handle non-finite values.
Results may differ from a plain program's by a relative error of at most 0.012.
Values sent between devices are 32-bit elements; how exact they have to be, the bound alone decides.
A program may use at most 256 MiB of HBM per device.

v0:
```python
import math

import jax
import jax.numpy as jnp
from jax import lax
from jax.sharding import PartitionSpec as P

HEAD_DIM = 64


EPSILON = 1e-06


def normalize(values):
    center = values - jnp.mean(values, axis=-1, keepdims=True)
    inverse = lax.rsqrt(jnp.mean(center * center, axis=-1, keepdims=True) + EPSILON)
    return (center * inverse, inverse)


def norm_back(grad_out, scale, normed, inverse):
    scaled = grad_out * scale
    return inverse * (
        scaled
        - jnp.mean(scaled, axis=-1, keepdims=True)
        - normed * jnp.mean(scaled * normed, axis=-1, keepdims=True)
    )


def gelu_slope(pre_act):
    cumul = 0.5 * (1.0 + lax.erf(pre_act * 0.7071067811865476))
    return cumul + pre_act * jnp.exp(-0.5 * pre_act * pre_act) * 0.3989422804014327


def cross_dot(left_side, right_side):
    return lax.dot_general(
        left_side, right_side, (((0,), (0,)), ((), ())), preferred_element_type=jnp.float32
    )


def back_dot(left_side, right_side):
    return lax.dot_general(
        left_side, right_side, (((1,), (1,)), ((), ())), preferred_element_type=jnp.float32
    )


def on_device(
    block_input,
    first_scale,
    first_shift,
    heads_weight,
    heads_bias,
    mixing_weight,
    mixing_bias,
    second_scale,
    second_shift,
    expand_weight,
    expand_bias,
    shrink_weight,
    shrink_bias,
    output_grad,
):
    images, length, width = block_input.shape
    local = heads_weight.shape[2]
    heads_here = local // HEAD_DIM
    total_rows = images * length
    factor = 1.0 / math.sqrt(HEAD_DIM)
    head_shape = (images, length, heads_here, HEAD_DIM)
    flat_in = block_input.reshape(total_rows, width).astype(jnp.float32)
    normed_one, inverse_one = normalize(flat_in)
    layer_one = (normed_one * first_scale + first_shift).astype(jnp.bfloat16)
    joined_weight = heads_weight.reshape(width, 3 * local)
    projected = jnp.dot(layer_one, joined_weight, preferred_element_type=jnp.float32).reshape(
        total_rows, 3, local
    )
    queries = (projected[:, 0] + heads_bias[0]).astype(jnp.bfloat16).reshape(head_shape)
    keys_all = projected[:, 1].astype(jnp.bfloat16).reshape(head_shape)
    values_all = (projected[:, 2] + heads_bias[1]).astype(jnp.bfloat16).reshape(head_shape)
    scores = (
        jnp.einsum("bqhd,bkhd->bhqk", queries, keys_all, preferred_element_type=jnp.float32)
        * factor
    )
    logsum = jax.nn.logsumexp(scores, axis=-1, keepdims=True)
    probs_low = jnp.exp(scores - logsum).astype(jnp.bfloat16)
    attended = jnp.einsum(
        "bhqk,bkhd->bqhd", probs_low, values_all, preferred_element_type=jnp.float32
    )
    attended = attended.astype(jnp.bfloat16).reshape(total_rows, local)
    mixed = lax.psum(jnp.dot(attended, mixing_weight, preferred_element_type=jnp.float32), "tensor")
    hidden_one = flat_in + mixed + mixing_bias
    normed_two, inverse_two = normalize(hidden_one)
    layer_two = (normed_two * second_scale + second_shift).astype(jnp.bfloat16)
    pre_act = jnp.dot(layer_two, expand_weight, preferred_element_type=jnp.float32) + expand_bias
    activated = jax.nn.gelu(pre_act, approximate=False).astype(jnp.bfloat16)
    shrunk = lax.psum(
        jnp.dot(activated, shrink_weight, preferred_element_type=jnp.float32), "tensor"
    )
    block_output = (
        (hidden_one + shrunk + shrink_bias).astype(jnp.bfloat16).reshape(images, length, width)
    )
    owner = lax.axis_index("tensor")
    share = images // lax.axis_size("tensor")

    def own_sum(rows_wide):
        picked = lax.dynamic_slice_in_dim(
            rows_wide.reshape(images, length, width), owner * share, share, 0
        )
        return jnp.sum(picked, axis=(0, 1))

    upstream = output_grad.reshape(total_rows, width)
    upstream_wide = upstream.astype(jnp.float32)
    shrink_grad = cross_dot(activated, upstream)
    shrink_bias_part = own_sum(upstream_wide)
    pre_grad = back_dot(upstream, shrink_weight) * gelu_slope(pre_act)
    pre_low = pre_grad.astype(jnp.bfloat16)
    expand_bias_grad = jnp.sum(pre_grad, axis=0)
    expand_grad = cross_dot(layer_two, pre_low)
    partial_two = back_dot(pre_low, expand_weight)
    second_scale_part = jnp.sum(partial_two * normed_two, axis=0)
    second_shift_part = jnp.sum(partial_two, axis=0)
    layer_two_grad = lax.psum(partial_two, "tensor")
    hidden_grad = upstream_wide + norm_back(layer_two_grad, second_scale, normed_two, inverse_two)
    mixing_bias_part = own_sum(hidden_grad)
    hidden_low = hidden_grad.astype(jnp.bfloat16)
    mixing_grad = cross_dot(attended, hidden_low)
    attended_grad = back_dot(hidden_low, mixing_weight).astype(jnp.bfloat16).reshape(head_shape)
    scores = (
        jnp.einsum("bqhd,bkhd->bhqk", queries, keys_all, preferred_element_type=jnp.float32)
        * factor
    )
    probs = jnp.exp(scores - logsum)
    values_grad = jnp.einsum(
        "bhqk,bqhd->bkhd",
        probs.astype(jnp.bfloat16),
        attended_grad,
        preferred_element_type=jnp.float32,
    )
    probs_grad = jnp.einsum(
        "bqhd,bkhd->bhqk", attended_grad, values_all, preferred_element_type=jnp.float32
    )
    row_dot = jnp.sum(probs * probs_grad, axis=-1, keepdims=True)
    score_low = (probs * (probs_grad - row_dot) * factor).astype(jnp.bfloat16)
    queries_grad = jnp.einsum(
        "bhqk,bkhd->bqhd", score_low, keys_all, preferred_element_type=jnp.float32
    )
    keys_grad = jnp.einsum(
        "bhqk,bqhd->bkhd", score_low, queries, preferred_element_type=jnp.float32
    )
    stacked = jnp.stack(
        [
            queries_grad.reshape(total_rows, local),
            keys_grad.reshape(total_rows, local),
            values_grad.reshape(total_rows, local),
        ],
        axis=1,
    )
    heads_bias_grad = jnp.stack([jnp.sum(stacked[:, 0], axis=0), jnp.sum(stacked[:, 2], axis=0)])
    stacked_low = stacked.astype(jnp.bfloat16).reshape(total_rows, 3 * local)
    heads_grad = cross_dot(layer_one, stacked_low).reshape(width, 3, local)
    partial_one = back_dot(stacked_low, joined_weight)
    first_scale_part = jnp.sum(partial_one * normed_one, axis=0)
    first_shift_part = jnp.sum(partial_one, axis=0)
    layer_one_grad = lax.psum(partial_one, "tensor")
    input_grad = hidden_grad + norm_back(layer_one_grad, first_scale, normed_one, inverse_one)
    input_grad = input_grad.astype(jnp.bfloat16).reshape(images, length, width)
    bias_heads_sum, bias_expand_sum = lax.psum((heads_bias_grad, expand_bias_grad), "dp")
    (
        first_scale_sum,
        first_shift_sum,
        second_scale_sum,
        second_shift_sum,
        mixing_bias_sum,
        shrink_bias_sum,
    ) = lax.psum(
        (
            first_scale_part,
            first_shift_part,
            second_scale_part,
            second_shift_part,
            mixing_bias_part,
            shrink_bias_part,
        ),
        ("dp", "tensor"),
    )
    weight_part = (
        lax.psum_scatter(heads_grad, "dp", scatter_dimension=0, tiled=True),
        lax.psum_scatter(mixing_grad, "dp", scatter_dimension=0, tiled=True),
        lax.psum_scatter(expand_grad, "dp", scatter_dimension=0, tiled=True),
        lax.psum_scatter(shrink_grad, "dp", scatter_dimension=0, tiled=True),
    )
    heads_full, mixing_full, expand_full, shrink_full = (
        lax.all_gather(weight_part[0], "dp", axis=0, tiled=True),
        lax.all_gather(weight_part[1], "dp", axis=0, tiled=True),
        lax.all_gather(weight_part[2], "dp", axis=0, tiled=True),
        lax.all_gather(weight_part[3], "dp", axis=0, tiled=True),
    )
    return (
        block_output,
        input_grad,
        heads_full,
        bias_heads_sum,
        mixing_full,
        mixing_bias_sum,
        second_scale_sum,
        second_shift_sum,
        expand_full,
        bias_expand_sum,
        shrink_full,
        shrink_bias_sum,
        first_scale_sum,
        first_shift_sum,
    )


def solution(mesh):
    placed = (
        P("dp", None, None),
        P(),
        P(),
        P(None, None, "tensor"),
        P(None, "tensor"),
        P("tensor", None),
        P(),
        P(),
        P(),
        P(None, "tensor"),
        P("tensor"),
        P("tensor", None),
        P(),
        P("dp", None, None),
    )
    return jax.shard_map(
        on_device,
        mesh=mesh,
        in_specs=placed,
        out_specs=(
            P("dp", None, None),
            P("dp", None, None),
            P(None, None, "tensor"),
            P(None, "tensor"),
            P("tensor", None),
            P(),
            P(),
            P(),
            P(None, "tensor"),
            P("tensor"),
            P("tensor", None),
            P(),
            P(),
            P(),
        ),
        check_vma=False,
    )
```

profile of v0, /device:TPU:0, one launch (start us, length us, event | category | flops | bytes accessed | tf_op | source)
XLA Modules:
  0.0 1360.9 jit_solution(9283532576933548809)
XLA Ops:
  15.1 4.8 add_convert_fusion.3
  25.6 4.6 copy.114
  30.2 6.5 fusion.29
  40.6 4.6 reshape.217
  45.2 5.1 copy.118
  50.3 4.1 reshape.221
  54.3 4.2 copy.120
  58.7 14.0 %multiply_reduce_fusion.1 = (f32[2,8,577]{2,1,0:T(8,128)S(1)}, f32[2,8,577,577]{2,3,1,0:T(8,128)}) fusion(bf16[2,577,8,64]{1,3,2,0:T(8,128)(2,1)} %copy.120, f32[2,577,8,64]{1,3,2,0:T(8,128)} %copy.118, f32[8,64]{1,0:T(8,128)S(1)} %add.150), kind=kOutput, calls=%fused_computation.6 | convolution fusion | flops 693664768 | bytes 24891520 | tf_op jit(solution)/shard_map/bqhd,bkhd->bhqk/dot_general | solution.py:79
  72.7 10.4 exponential_reduce_fusion
  83.1 4.6 reshape.216
  87.7 5.0 copy.116
  94.8 12.8 fusion.48
  110.0 4.4 reshape.206
  114.4 4.9 fusion.70
  122.4 5.0 reshape.212
  132.1 110.1 %all-reduce.7.cloned.1.call-done = f32[1154,1024]{1,0:T(8,128)} async-done(((f32[1154,1024]{1,0:T(8,128)}), f32[1154,1024]{1,0:T(8,128)}) %all-reduce.7.cloned.1.call-update) | async-done | bytes 4726800 | tf_op jit(solution)/shard_map/psum | solution.py:88
  242.2 4.4 fusion.63
  250.5 28.3 %fusion.7 = (bf16[1154,2048]{1,0:T(8,128)(2,1)}, f32[1154,2048]{1,0:T(8,128)}) fusion(f32[2048]{0:T(1024)S(1)} %copy-done.44, bf16[1024,2048]{1,0:T(8,128)(2,1)S(1)} %copy-done.42, f32[1154,1024]{1,0:T(8,128)S(1)} %get-tuple-element.91, f32[1024]{0:T(1024)S(1)} %copy-done.45, f32[1024]{0:T(1024)S(1)} %copy-done.35, f32[1154]{0:T(1024)S(1)} %add_rsqrt_fusion.1, ...), kind=kOutput, calls=%fused_computation.14 | convolution fusion | flops 5002119168 | bytes 23127056 | tf_op jit(solution)/shard_map/dot_general | solution.py:92
  278.8 10.9 fusion.69
  291.9 6.8 fusion.33
  298.8 120.1 %all-reduce.9.cloned.1.call-done = f32[1154,1024]{1,0:T(8,128)} async-done(((f32[1154,1024]{1,0:T(8,128)}), f32[1154,1024]{1,0:T(8,128)}) %all-reduce.9.cloned.1.call-update) | async-done | bytes 4726800 | tf_op jit(solution)/shard_map/psum | solution.py:120
  418.9 7.2 multiply_reduce_fusion.3
  437.3 4.1 copy.125
  441.4 13.8 %fusion.72 = f32[2,8,577,577]{2,3,1,0:T(8,128)} fusion(bf16[2,577,8,64]{1,3,2,0:T(8,128)(2,1)} %copy.125, bf16[2,577,8,64]{1,3,2,0:T(8,128)(2,1)S(1)} %copy-done.8), kind=kOutput, calls=%fused_computation.107 | convolution fusion | flops 681838592 | bytes 23670848 | tf_op jit(solution)/shard_map/bqhd,bkhd->bhqk/dot_general | solution.py:137
  455.3 27.6 %fusion.66 = (f32[8,64]{1,0:T(8,128)S(1)}, bf16[2,577,8,64]{1,3,2,0:T(8,128)(2,1)}) fusion(bf16[2,577,8,64]{1,3,2,0:T(8,128)(2,1)} %copy.120, f32[2,8,577,577]{2,3,1,0:T(8,128)} %fusion.72, f32[2,8,577]{2,1,0:T(8,128)S(1)} %copy-done.26, f32[2,8,577,577]{2,3,1,0:T(8,128)} %get-tuple-element.95, bf16[2,577,8,64]{1,3,2,0:T(8,128)(2,1)} %copy.125, ...), kind=kOutput, calls=%fused_computation.103 | convolution fusion | flops 1412809728 | bytes 47380672 | tf_op jit(solution)/shard_map/bhqk,bkhd->bqhd/dot_general | solution.py:142
  486.8 4.2 reshape.218
  491.1 27.1 %fusion.39 = bf16[2,577,8,64]{1,3,2,0:T(8,128)(2,1)} fusion(f32[2,8,577,577]{2,3,1,0:T(8,128)} %fusion.72, f32[2,8,577]{2,1,0:T(8,128)S(1)} %copy-done.26, f32[2,8,577,577]{2,3,1,0:T(8,128)} %get-tuple-element.95, bf16[2,577,8,64]{1,3,2,0:T(8,128)(2,1)} %copy.125, bf16[2,577,8,64]{1,3,2,0:T(8,128)(2,1)S(1)} %copy-done.8, f32[2,577,8,64]{1,3,2,0:T(8,128)} %copy.118, ...), kind=kOutput, calls=%fused_computation.72 | convolution fusion | flops 1412810240 | bytes 48562368 | tf_op jit(solution)/shard_map/bhqk,bqhd->bkhd/dot_general | solution.py:145
  522.2 4.2 reshape.219
  526.4 11.1 fusion.65
  543.9 9.7 fusion.27
  554.4 11.4 fusion.31
  567.7 10.6 fusion.73
  579.2 10.1 fusion.71
  589.3 5.7 convolution_bitcast_fusion
  595.0 44.0 %reduce-scatter.5.cloned.1.call-done = f32[64,3,512]{2,0,1:T(8,128)} async-done(((f32[1024,3,512]{2,0,1:T(8,128)}), f32[64,3,512]{2,0,1:T(8,128)}) %reduce-scatter.5.cloned.1.call-update) | async-done | bytes 393232 | tf_op jit(solution)/shard_map/reduce_scatter | solution.py:185
  639.1 107.1 %reduce-scatter.9.cloned.1.call-done = f32[64,2048]{1,0:T(8,128)} async-done(((f32[1024,2048]{1,0:T(8,128)}), f32[64,2048]{1,0:T(8,128)}) %reduce-scatter.9.cloned.1.call-update) | async-done | bytes 524304 | tf_op jit(solution)/shard_map/reduce_scatter | solution.py:187
  746.2 107.5 %reduce-scatter.11.cloned.1.call-done = f32[128,1024]{1,0:T(8,128)} async-done(((f32[2048,1024]{1,0:T(8,128)}), f32[128,1024]{1,0:T(8,128)}) %reduce-scatter.11.cloned.1.call-update) | async-done | bytes 524304 | tf_op jit(solution)/shard_map/reduce_scatter | solution.py:188
  857.4 5.1 reshape.211
  862.6 61.0 %all-reduce.1 = (f32[2,512]{1,0:T(2,128)}, f32[2048]{0:T(1024)}) all-reduce(f32[2,512]{1,0:T(2,128)S(1)} %pad_maximum_fusion, f32[2048]{0:T(1024)S(1)} %copy-done.37), channel_id=1, replica_groups=mesh['dp'=16,'tensor'=2] {'dp'}, use_global_device_ids=true, to_apply=%region_18.0 | all-reduce | flops 3072 | bytes 24576 | tf_op jit(solution)/shard_map/psum | solution.py:165
  925.6 195.1 %all-reduce.11.cloned.1.call-done = (f32[1154,1024]{1,0:T(8,128)}, f32[1154,1024]{1,0:T(8,128)}) async-done(((f32[1154,1024]{1,0:T(8,128)}, f32[1154,1024]{1,0:T(8,128)}), (f32[1154,1024]{1,0:T(8,128)}, f32[1154,1024]{1,0:T(8,128)})) %all-reduce.11.cloned.1.call-update) | async-done | bytes 9453584 | tf_op jit(solution)/shard_map/psum | solution.py:94
  1120.7 6.4 multiply_reduce_fusion.2
  1128.5 4.4 add_convert_fusion
  1138.8 5.0 add_convert_fusion.1
  1149.9 42.4 %all-reduce = (f32[1024]{0:T(1024)}, f32[1024]{0:T(1024)}, f32[1024]{0:T(1024)}, f32[1024]{0:T(1024)}, f32[1024]{0:T(1024)}, /*index=5*/f32[1024]{0:T(1024)}) all-reduce(f32[1024]{0:T(1024)S(1)} %dynamic-slice_reduce_fusion, f32[1024]{0:T(1024)S(1)} %copy-done.33, ...), channel_id=1, replica_groups=mesh['dp'=16,'tensor'=2] {'dp','tensor'}, use_global_device_ids=true, to_apply=%region_21.0 | all-reduce | flops 6144 | bytes 49152 | tf_op jit(solution)/shard_map/psum | solution.py:173
  1192.3 69.0 %all-gather.9.cloned.1.call-done = f32[1024,2048]{1,0:T(8,128)} async-done(((f32[64,2048]{1,0:T(8,128)}), f32[1024,2048]{1,0:T(8,128)}) %all-gather.9.cloned.1.call-update) | async-done | bytes 8388624 | tf_op jit(solution)/shard_map/all_gather | solution.py:193
  1261.3 75.1 %all-gather.11.cloned.1.call-done = f32[2048,1024]{1,0:T(8,128)} async-done(((f32[128,1024]{1,0:T(8,128)}), f32[2048,1024]{1,0:T(8,128)}) %all-gather.11.cloned.1.call-update) | async-done | bytes 8388624 | tf_op jit(solution)/shard_map/all_gather | solution.py:194
  1336.4 6.9 copy.172
  1345.0 4.3 copy.174
  (178 shorter events, 90.7 us)
Async XLA Ops:
  7.2 107.2 %copy-start = (bf16[512,1024]{1,0:T(8,128)(2,1)S(1)}, bf16[512,1024]{1,0:T(8,128)(2,1)}, u32[]{:S(2)}) copy-start(bf16[512,1024]{1,0:T(8,128)(2,1)} %param.19) | copy-start | bytes 3145732
  7.2 7.9 copy-start.31
  7.2 7.9 copy-start.41
  7.2 235.0 %all-reduce.7.cloned.1.call-start = ((), (), s32[]{:S(2)}) async-start(), calls=%async_computation.4 | async-start | bytes 9502720 | tf_op jit(solution)/shard_map/psum | solution.py:88
  50.3 8.3 copy-start.40
  58.7 14.0 %copy-start.29 = (f32[8,64]{1,0:T(8,128)}, f32[8,64]{1,0:T(8,128)S(1)}, u32[]{:S(2)}) copy-start(f32[8,64]{1,0:T(8,128)S(1)} %add.150) | copy-start | bytes 6148
  83.1 11.6 copy-start.25
  94.7 12.8 copy-start.7
  119.3 299.5 %all-reduce.9.cloned.1.call-start = ((), (), s32[]{:S(2)}) async-start(), calls=%async_computation.5 | async-start | bytes 9502720 | tf_op jit(solution)/shard_map/psum | solution.py:120
  127.4 114.8 %copy-start.38 = (f32[1024]{0:T(1024)S(1)}, f32[1024]{0:T(1024)}, u32[]{:S(2)}) copy-start(f32[1024]{0:T(1024)} %param.20) | copy-start | bytes 12292
  246.6 32.2 %copy-start.2 = (f32[1154,1024]{1,0:T(8,128)}, f32[1154,1024]{1,0:T(8,128)S(1)}, u32[]{:S(2)}) copy-start(f32[1154,1024]{1,0:T(8,128)S(1)} %get-tuple-element.91) | copy-start | bytes 14180356
  250.5 175.5 %copy-start.27 = (f32[1154]{0:T(1024)}, f32[1154]{0:T(1024)S(1)}, u32[]{:S(2)}) copy-start(f32[1154]{0:T(1024)S(1)} %add_rsqrt_fusion.1) | copy-start | bytes 13852
  250.5 28.3 %copy-start.10 = (bf16[1154,1024]{1,0:T(8,128)(2,1)S(1)}, bf16[1154,1024]{1,0:T(8,128)(2,1)}, u32[]{:S(2)}) copy-start(bf16[1154,1024]{1,0:T(8,128)(2,1)} %reshape.208) | copy-start | bytes 7090180
  250.5 28.3 %copy-start.43 = (bf16[2048,1024]{1,0:T(8,128)(2,1)S(1)}, bf16[2048,1024]{1,0:T(8,128)(2,1)}, u32[]{:S(2)}) copy-start(bf16[2048,1024]{1,0:T(8,128)(2,1)} %param.25) | copy-start | bytes 12582916
  298.8 279.6 %reduce-scatter.7.cloned.1.call-start = ((), (), s32[]{:S(2)}) async-start(), calls=%async_computation.8 | async-start | bytes 2228224 | tf_op jit(solution)/shard_map/reduce_scatter | solution.py:186
  418.9 7.2 copy-start.6
  434.6 6.8 copy-start.8
  441.3 13.9 %copy-start.26 = (f32[2,8,577]{2,1,0:T(8,128)S(1)}, f32[2,8,577]{2,1,0:T(8,128)}, u32[]{:S(2)}) copy-start(f32[2,8,577]{2,1,0:T(8,128)} %copy-done.25) | copy-start | bytes 110788
  441.3 197.7 %reduce-scatter.5.cloned.1.call-start = ((), (), s32[]{:S(2)}) async-start(), calls=%async_computation.6 | async-start | bytes 6684672 | tf_op jit(solution)/shard_map/reduce_scatter | solution.py:185
  482.9 8.2 copy-start.30
  518.1 8.3 copy-start.9
  553.7 192.5 %reduce-scatter.9.cloned.1.call-start = ((), (), s32[]{:S(2)}) async-start(), calls=%async_computation.10 | async-start | bytes 8912896 | tf_op jit(solution)/shard_map/reduce_scatter | solution.py:187
  565.8 287.9 %reduce-scatter.11.cloned.1.call-start = ((), (), s32[]{:S(2)}) async-start(), calls=%async_computation.12 | async-start | bytes 8912896 | tf_op jit(solution)/shard_map/reduce_scatter | solution.py:188
  578.3 347.2 %all-gather.7.cloned.1.call-start = ((), (), s32[]{:S(2)}) async-start(), calls=%async_computation.9 | async-start | bytes 2228224 | tf_op jit(solution)/shard_map/all_gather | solution.py:192
  579.1 10.2 copy-start.22
  579.1 10.2 copy-start.23
  579.1 541.6 %all-reduce.11.cloned.1.call-start = ((), (), s32[]{:S(2)}) async-start(), calls=%async_computation.14 | async-start | bytes 19005440 | tf_op jit(solution)/shard_map/psum | solution.py:94
  579.2 10.1 copy-start.18
  579.2 10.1 copy-start.24
  594.9 258.9 %copy-start.20 = (f32[2,577]{0,1:T(8,128)S(1)}, f32[2,577]{0,1:T(8,128)}, u32[]{:S(2)}) copy-start(f32[2,577]{0,1:T(8,128)} %copy-done.19) | copy-start | bytes 13852
  594.9 259.0 %copy-start.16 = (f32[2,577]{0,1:T(8,128)S(1)}, f32[2,577]{0,1:T(8,128)}, u32[]{:S(2)}) copy-start(f32[2,577]{0,1:T(8,128)} %copy-done.15) | copy-start | bytes 13852
  594.9 259.3 %copy-start.12 = (bf16[2,577,1024]{2,0,1:T(2,128)(2,1)S(1)}, bf16[2,577,1024]{2,0,1:T(2,128)(2,1)}, u32[]{:S(2)}) copy-start(bf16[2,577,1024]{2,0,1:T(2,128)(2,1)} %param.27) | copy-start | bytes 7090180
  595.0 597.3 %all-gather.5.cloned.1.call-start = ((), (), s32[]{:S(2)}) async-start(), calls=%async_computation.7 | async-start | bytes 6684672 | tf_op jit(solution)/shard_map/all_gather | solution.py:191
  639.0 622.2 %all-gather.9.cloned.1.call-start = ((), (), s32[]{:S(2)}) async-start(), calls=%async_computation.11 | async-start | bytes 8912896 | tf_op jit(solution)/shard_map/all_gather | solution.py:193
  746.2 590.2 %all-gather.11.cloned.1.call-start = ((), (), s32[]{:S(2)}) async-start(), calls=%async_computation.13 | async-start | bytes 8912896 | tf_op jit(solution)/shard_map/all_gather | solution.py:194
  857.4 5.3 copy-start.37
  857.4 263.4 %copy-start.32 = (f32[1024]{0:T(1024)S(1)}, f32[1024]{0:T(1024)}, u32[]{:S(2)}) copy-start(f32[1024]{0:T(1024)} %param.15) | copy-start | bytes 12292
  857.4 269.8 %slice-start = ((s8[4751360]{0:T(1024)(128)(4,1)}), s8[557056]{0:T(1024)(128)(4,1)S(1)}, s32[]{:S(2)}) async-start(s8[4751360]{0:T(1024)(128)(4,1)} %bitcast.64), calls=%async_computation.15 | async-start | bytes 1114112
  1120.7 6.5 slice-start.1
  1120.7 7.8 copy-start.5
  1132.8 6.0 copy-start.39
  1143.9 6.0 copy-start.33
  1143.9 6.0 copy-start.34
  1336.4 6.9 copy-start.21
  1336.4 8.6 copy-start.13
  1343.3 5.9 slice-start.2
  1345.0 5.8 slice-start.3
  1345.0 9.2 copy-start.1
  (15 other events, 34.8 us)
Sparse Core Ops, SparseCore 0:
  119.5 122.6 all-reduce.6
  298.9 119.9 all-reduce.8
  441.5 61.7 reduce-scatter.6
  553.8 85.1 reduce-scatter.4
  643.5 102.5 reduce-scatter.8
  750.6 103.0 reduce-scatter.10
  855.9 41.3 all-gather.6
  899.9 220.8 all-reduce.10
  1122.9 63.2 all-gather.4
  1188.2 73.0 all-gather.8
  1263.5 72.8 all-gather.10
where the time goes:
time: 1370 us; the launch traced here: 1360 us
  waiting for transfers between devices  829 us (61%)
  matrix products  216 us (16%)
  local copies, waits for them, and re-layouts  137 us (10%)
  blocking collectives  103 us (8%)
  other arithmetic  60.7 us (4%)
  between operations  14.6 us (1%)
    psum x1, waiting for transfers between devices, on_device(): lax.psum(jnp.dot(activated, shrink_weight, preferred_element_type=jnp.flo...  195 us
    psum x1, waiting for transfers between devices, on_device(): layer_two_grad = lax.psum(partial_two, 'tensor')  120 us
    psum x1, waiting for transfers between devices, on_device(): lax.psum(jnp.dot(attended, mixing_weight, preferred_element_type=jnp.floa...  110 us
    reduce_scatter x1, waiting for transfers between devices, on_device(): lax.psum_scatter(shrink_grad, 'dp', scatter_dimension=0, tiled=True)  108 us
    reduce_scatter x1, waiting for transfers between devices, on_device(): lax.psum_scatter(expand_grad, 'dp', scatter_dimension=0, tiled=True)  107 us
    all_gather x1, waiting for transfers between devices, on_device(): lax.all_gather(weight_part[3], 'dp', axis=0, tiled=True)  75.1 us
    all_gather x1, waiting for transfers between devices, on_device(): lax.all_gather(weight_part[2], 'dp', axis=0, tiled=True)  69 us
    psum x1, blocking collectives, on_device(): lax.psum((heads_bias_grad, expand_bias_grad), 'dp')  61 us
  transfers between devices with their start and end apart: 11, of which 8 were waited for; matrix products, arithmetic and copies ran while one was open for 15% of the time, Pallas kernels for 0%

commit v1 on v0

v1 whole, which is shorter than its diff:
```python
import functools
import math

import jax
import jax.numpy as jnp
from jax import lax
from jax.experimental import pallas as pl
from jax.experimental.pallas import tpu as pltpu
from jax.sharding import PartitionSpec as P

HEAD_DIM = 64
PAIR = 2 * HEAD_DIM
EPSILON = 1e-06
QUERIES = 128
LANES = 128
f32 = jnp.float32
bf16 = jnp.bfloat16


def dot(left, right):
    return jnp.dot(left, right, preferred_element_type=f32)


def nt_dot(left, right):
    return lax.dot_general(left, right, (((1,), (1,)), ((), ())), preferred_element_type=f32)


def tn_dot(left, right):
    return lax.dot_general(left, right, (((0,), (0,)), ((), ())), preferred_element_type=f32)


def cost(flops, nbytes, trans=0):
    return pl.CostEstimate(flops=flops, bytes_accessed=nbytes, transcendentals=trans)


def normalize(values):
    center = values - jnp.mean(values, axis=-1, keepdims=True)
    inverse = lax.rsqrt(jnp.mean(center * center, axis=-1, keepdims=True) + EPSILON)
    return center * inverse, inverse


def norm_back(grad_out, scale, normed, inverse):
    scaled = grad_out * scale
    return inverse * (
        scaled
        - jnp.mean(scaled, axis=-1, keepdims=True)
        - normed * jnp.mean(scaled * normed, axis=-1, keepdims=True)
    )


def pad_rows(target, source):
    rows, length = target.shape[0], source.shape[0]
    edge = length // 8 * 8
    if edge < rows:
        target[pl.ds(edge, rows - edge), :] = jnp.zeros((rows - edge, target.shape[1]), f32)
    target[pl.ds(0, length), :] = source.astype(f32)


def stack_heads(block, scale):
    lane = lax.broadcasted_iota(jnp.int32, block.shape, 1)
    block = block * jnp.asarray(scale, block.dtype)
    zero = jnp.zeros_like(block)
    return jnp.concatenate(
        [jnp.where(lane < HEAD_DIM, block, zero), jnp.where(lane < HEAD_DIM, zero, block)], axis=0
    )


def unstack_heads(stacked):
    return jnp.concatenate([stacked[:HEAD_DIM, :QUERIES], stacked[HEAD_DIM:, QUERIES:]], axis=0)


def fill_rows(target, source):
    rows = source.shape[0]
    target[pl.ds(0, rows), :] = source
    rest = target.shape[0] - rows
    if rest > 0:
        target[pl.ds(rows, rest), :] = jnp.zeros((rest, target.shape[1]), target.dtype)


def attend_kernel(
    length, chunks, input_ref, weight_ref, bias_ref, scale_ref, shift_ref,
    layer_ref, qkv_ref, out_ref, wide_ref, logsum_ref, block, queries, result,
):
    rows = layer_ref.shape[0]

    @pl.when(pl.program_id(0) == 0)
    def _():
        pad_rows(block, input_ref[...])
        normed, _ = normalize(block[...])
        layer_ref[...] = (normed * scale_ref[...] + shift_ref[...]).astype(bf16)

    qkv_ref[...] = (dot(layer_ref[...], weight_ref[...]) + bias_ref[...]).astype(bf16)
    fill_rows(queries, qkv_ref[:, 0:PAIR])
    keys = qkv_ref[:, PAIR : 2 * PAIR]
    values = qkv_ref[:, 2 * PAIR : 3 * PAIR]

    def body(step, carry):
        at = pl.ds(pl.multiple_of(step * QUERIES, QUERIES), QUERIES)
        stacked = stack_heads(queries[at, :], 1.0 / math.sqrt(HEAD_DIM))
        scores = nt_dot(keys, stacked)
        row = lax.broadcasted_iota(jnp.int32, scores.shape, 0)
        scores = jnp.where(row < length, scores, -1e30)
        top = jnp.max(scores, axis=0, keepdims=True)
        powers = jnp.exp(scores - top)
        total = jnp.sum(powers, axis=0, keepdims=True)
        probs = (powers * (1.0 / total)).astype(bf16)
        logsum_ref[step] = top + jnp.log(total)
        mixed = unstack_heads(tn_dot(values, probs))
        result[at, :] = mixed.T.astype(bf16)
        return carry

    lax.fori_loop(0, chunks, body, 0, unroll=True)
    low = result[pl.ds(0, rows), :]
    out_ref[...] = low
    wide_ref[...] = low.astype(f32)


def attend(image, rows, block_input, joined, joined_bias, scale, shift):
    _, length, width = block_input.shape
    pairs = joined.shape[1] // (3 * PAIR)
    chunks = -(-rows // QUERIES)
    pair_block = pl.BlockSpec((rows, PAIR), lambda j: (0, j))
    vector = pl.BlockSpec((1, width), lambda j: (0, 0))
    return pl.pallas_call(
        functools.partial(attend_kernel, length, chunks),
        grid=(pairs,),
        in_specs=[
            pl.BlockSpec((None, length, width), lambda j: (image, 0, 0)),
            pl.BlockSpec((width, 3 * PAIR), lambda j: (0, j)),
            pl.BlockSpec((1, 3 * PAIR), lambda j: (0, j)),
            vector,
            vector,
        ],
        out_specs=[
            pl.BlockSpec((rows, width), lambda j: (0, 0)),
            pl.BlockSpec((rows, 3 * PAIR), lambda j: (0, j)),
            pair_block,
            pair_block,
            pl.BlockSpec((None, chunks, 1, 2 * QUERIES), lambda j: (j, 0, 0, 0)),
        ],
        out_shape=[
            jax.ShapeDtypeStruct((rows, width), bf16),
            jax.ShapeDtypeStruct((rows, pairs * 3 * PAIR), bf16),
            jax.ShapeDtypeStruct((rows, pairs * PAIR), bf16),
            jax.ShapeDtypeStruct((rows, pairs * PAIR), f32),
            jax.ShapeDtypeStruct((pairs, chunks, 1, 2 * QUERIES), f32),
        ],
        scratch_shapes=[
            pltpu.VMEM((rows, width), f32),
            pltpu.VMEM((chunks * QUERIES, PAIR), bf16),
            pltpu.VMEM((chunks * QUERIES, PAIR), bf16),
        ],
        cost_estimate=cost(10_000_000_000, 10_000_000),
        name="attend",
    )(block_input, joined, joined_bias, scale, shift)


def attend_back_kernel(
    length, chunks, pairs, own_ref, other_ref, hidden_ref, upstream_ref, mixing_ref, qkv_ref,
    logsum_ref, joined_ref, input_ref, scale_ref,
    grad_ref, low_ref, out_ref, qbias_ref, vbias_ref, partial_ref, sums_ref, first_ref,
    block, queries, grads, query_out, key_sum, value_sum, stacked_all,
):
    pair = pl.program_id(0)
    rows = qkv_ref.shape[0]
    factor = 1.0 / math.sqrt(HEAD_DIM)

    @pl.when(pair == 0)
    def _():
        normed, inverse = normalize(hidden_ref[...])
        layer_grad = own_ref[...] + other_ref[...]
        upstream = upstream_ref[...].astype(f32)
        grad = upstream + norm_back(layer_grad, scale_ref[...], normed, inverse)
        grad_ref[...] = grad
        low_ref[...] = grad.astype(bf16)
        sums_ref[0:1, :] = jnp.sum(layer_grad * normed, axis=0, keepdims=True)
        sums_ref[1:2, :] = jnp.sum(layer_grad, axis=0, keepdims=True)
        sums_ref[2:3, :] = jnp.sum(grad, axis=0, keepdims=True)
        sums_ref[3:4, :] = jnp.sum(upstream, axis=0, keepdims=True)

    fill_rows(queries, qkv_ref[:, 0:PAIR])
    fill_rows(grads, nt_dot(low_ref[...], mixing_ref[...]).astype(bf16))
    keep = lax.broadcasted_iota(jnp.int32, (rows, PAIR), 0) < length
    empty = jnp.zeros((rows, PAIR), bf16)
    keys = jnp.where(keep, qkv_ref[:, PAIR : 2 * PAIR], empty)
    values = jnp.where(keep, qkv_ref[:, 2 * PAIR : 3 * PAIR], empty)
    key_sum[...] = jnp.zeros_like(key_sum)
    value_sum[...] = jnp.zeros_like(value_sum)

    def body(step, bias):
        at = pl.ds(pl.multiple_of(step * QUERIES, QUERIES), QUERIES)
        stacked = stack_heads(queries[at, :], factor)
        upstream = stack_heads(grads[at, :], 1.0)
        probs = jnp.exp(nt_dot(keys, stacked) - logsum_ref[step])
        probs_grad = nt_dot(values, upstream)
        value_sum[...] += dot(probs.astype(bf16), upstream)
        product = probs * probs_grad
        row_dot = jnp.sum(product, axis=0, keepdims=True)
        score = (product - probs * row_dot).astype(bf16)
        key_sum[...] += dot(score, stacked)
        query_grad = unstack_heads(tn_dot(keys, score)).T * factor
        query_out[at, :] = query_grad.astype(bf16)
        return bias + jnp.sum(query_grad, axis=0, keepdims=True)

    qbias_ref[...] = lax.fori_loop(0, chunks, body, jnp.zeros((1, PAIR), f32), unroll=True)
    wide = jnp.zeros((rows, PAIR), f32)
    value_grad = jnp.where(keep, value_sum[...], wide)
    vbias_ref[...] = jnp.sum(value_grad, axis=0, keepdims=True)
    out_ref[:, 0:PAIR] = query_out[pl.ds(0, rows), :]
    out_ref[:, PAIR : 2 * PAIR] = jnp.where(keep, key_sum[...], wide).astype(bf16)
    out_ref[:, 2 * PAIR : 3 * PAIR] = value_grad.astype(bf16)
    stacked_all[:, pl.ds(pl.multiple_of(pair * 3 * PAIR, LANES), 3 * PAIR)] = out_ref[...]

    @pl.when(pair == pairs - 1)
    def _():
        partial = nt_dot(stacked_all[...], joined_ref[...])
        partial_ref[...] = partial
        pad_rows(block, input_ref[...])
        normed, _ = normalize(block[...])
        first_ref[0:1, :] = jnp.sum(partial * normed, axis=0, keepdims=True)
        first_ref[1:2, :] = jnp.sum(partial, axis=0, keepdims=True)


def attend_back(image, own, other, hidden, upstream, mixing, qkv, logsum, joined, block_input, scale):
    rows, width = own.shape
    length = block_input.shape[1]
    pairs = joined.shape[1] // (3 * PAIR)
    chunks = -(-rows // QUERIES)
    full = pl.BlockSpec((rows, width), lambda j: (0, 0))
    stack = pl.BlockSpec((rows, 3 * PAIR), lambda j: (0, j))
    bias = pl.BlockSpec((1, PAIR), lambda j: (0, j))
    return pl.pallas_call(
        functools.partial(attend_back_kernel, length, chunks, pairs),
        grid=(pairs,),
        in_specs=[
            full,
            full,
            full,
            full,
            pl.BlockSpec((PAIR, width), lambda j: (j, 0)),
            stack,
            pl.BlockSpec((None, chunks, 1, 2 * QUERIES), lambda j: (j, 0, 0, 0)),
            pl.BlockSpec(joined.shape, lambda j: (0, 0)),
            pl.BlockSpec((None, length, width), lambda j: (image, 0, 0)),
            pl.BlockSpec((1, width), lambda j: (0, 0)),
        ],
        out_specs=[
            full,
            full,
            stack,
            bias,
            bias,
            full,
            pl.BlockSpec((4, width), lambda j: (0, 0)),
            pl.BlockSpec((2, width), lambda j: (0, 0)),
        ],
        out_shape=[
            jax.ShapeDtypeStruct((rows, width), f32),
            jax.ShapeDtypeStruct((rows, width), bf16),
            jax.ShapeDtypeStruct((rows, pairs * 3 * PAIR), bf16),
            jax.ShapeDtypeStruct((1, pairs * PAIR), f32),
            jax.ShapeDtypeStruct((1, pairs * PAIR), f32),
            jax.ShapeDtypeStruct((rows, width), f32),
            jax.ShapeDtypeStruct((4, width), f32),
            jax.ShapeDtypeStruct((2, width), f32),
        ],
        scratch_shapes=[pltpu.VMEM((rows, width), f32)]
        + [pltpu.VMEM((chunks * QUERIES, PAIR), bf16)] * 3
        + [pltpu.VMEM((rows, PAIR), f32)] * 2
        + [pltpu.VMEM((rows, pairs * 3 * PAIR), bf16)],
        cost_estimate=cost(12_000_000_000, 20_000_000),
        name="attend_back",
    )(own, other, hidden, upstream, mixing, qkv, logsum, joined, block_input, scale)


def gather_kernel(place_ref, own_ref, near_ref, far_ref, out_ref):
    half = near_ref.shape[0]
    own = place_ref[0] * 2 * half
    other = (1 - place_ref[0]) * 2 * half
    out_ref[pl.ds(pl.multiple_of(own, LANES), 2 * half), :] = own_ref[...]
    near = other + place_ref[1] * half
    far = other + (1 - place_ref[1]) * half
    out_ref[pl.ds(pl.multiple_of(near, LANES), half), :] = near_ref[...].astype(bf16)
    out_ref[pl.ds(pl.multiple_of(far, LANES), half), :] = far_ref[...].astype(bf16)


def gather_weight(place, own, near, far):
    whole = pl.BlockSpec(memory_space=pltpu.VMEM)
    return pl.pallas_call(
        gather_kernel,
        in_specs=[pl.BlockSpec(memory_space=pltpu.SMEM), whole, whole, whole],
        out_specs=whole,
        out_shape=jax.ShapeDtypeStruct((2 * own.shape[0], own.shape[1]), bf16),
        cost_estimate=cost(1_000_000, 6_000_000),
        name="gather_weight",
    )(place, own, near, far)


def feed_kernel(
    place_ref, input_ref, own_ref, other_ref, mixing_ref, mixing_bias_ref, scale_ref, shift_ref,
    upstream_ref, expand_ref, bias_ref, shrink_ref,
    hidden_ref, layer_ref, grad_ref, act_ref, low_ref, sum_ref, shrunk_ref, partial_ref,
    both, block,
):
    tile = pl.program_id(0)
    rows = layer_ref.shape[0]

    @pl.when(tile == 0)
    def _():
        width = own_ref.shape[1]
        own = place_ref[0] * width
        other = (1 - place_ref[0]) * width
        both[:, pl.ds(pl.multiple_of(own, LANES), width)] = own_ref[...]
        both[:, pl.ds(pl.multiple_of(other, LANES), width)] = other_ref[...].astype(bf16)
        pad_rows(block, input_ref[...])
        mixed = block[...] + dot(both[...], mixing_ref[...]) + mixing_bias_ref[...]
        hidden_ref[...] = mixed
        normed, _ = normalize(mixed)
        layer_ref[...] = (normed * scale_ref[...] + shift_ref[...]).astype(bf16)
        pad_rows(block, upstream_ref[...])
        grad_ref[...] = block[...].astype(bf16)

    cut = (rows // 32) * 16
    expand, shrink, bias = expand_ref[...], shrink_ref[...], bias_ref[...]
    total = jnp.zeros(bias.shape, f32)
    for low, high in ((0, cut), (cut, rows)):
        part = pl.ds(low, high - low)
        pre_act = dot(layer_ref[part, :], expand) + bias
        back = nt_dot(grad_ref[part, :], shrink)
        cumul = 0.5 * (1.0 + lax.erf(pre_act * 0.7071067811865476))
        slope = cumul + pre_act * jnp.exp(-0.5 * pre_act * pre_act) * 0.3989422804014327
        act = (pre_act * cumul).astype(bf16)
        act_ref[part, :] = act
        pre_grad = back * slope
        total = total + jnp.sum(pre_grad, axis=0, keepdims=True)
        pre_low = pre_grad.astype(bf16)
        low_ref[part, :] = pre_low
        shrunk = dot(act, shrink)
        partial = nt_dot(pre_low, expand)

        @pl.when(tile == 0)
        def _():
            shrunk_ref[part, :] = shrunk
            partial_ref[part, :] = partial

        @pl.when(tile > 0)
        def _():
            shrunk_ref[part, :] += shrunk
            partial_ref[part, :] += partial

    sum_ref[...] = total


def feed(
    image, place, block_input, own, other, mixing, mixing_bias, scale, shift, upstream,
    expand, bias, shrink,
):
    rows = own.shape[0]
    _, length, width = block_input.shape
    hidden = expand.shape[1]
    tile = math.gcd(hidden, 1024)
    full = pl.BlockSpec((rows, width), lambda j: (0, 0))
    half = pl.BlockSpec((rows, own.shape[1]), lambda j: (0, 0))
    vector = pl.BlockSpec((1, width), lambda j: (0, 0))
    picture = pl.BlockSpec((None, length, width), lambda j: (image, 0, 0))
    block = pl.BlockSpec((rows, tile), lambda j: (0, j))
    row = pl.BlockSpec((1, tile), lambda j: (0, j))
    return pl.pallas_call(
        feed_kernel,
        grid=(hidden // tile,),
        in_specs=[
            pl.BlockSpec(memory_space=pltpu.SMEM),
            picture,
            half,
            half,
            pl.BlockSpec(mixing.shape, lambda j: (0, 0)),
            vector,
            vector,
            vector,
            picture,
            pl.BlockSpec((width, tile), lambda j: (0, j)),
            row,
            pl.BlockSpec((tile, width), lambda j: (j, 0)),
        ],
        out_specs=[full, full, full, block, block, row, full, full],
        out_shape=[
            jax.ShapeDtypeStruct((rows, width), f32),
            jax.ShapeDtypeStruct((rows, width), bf16),
            jax.ShapeDtypeStruct((rows, width), bf16),
            jax.ShapeDtypeStruct((rows, hidden), bf16),
            jax.ShapeDtypeStruct((rows, hidden), bf16),
            jax.ShapeDtypeStruct((1, hidden), f32),
            jax.ShapeDtypeStruct((rows, width), f32),
            jax.ShapeDtypeStruct((rows, width), f32),
        ],
        scratch_shapes=[pltpu.VMEM((rows, width), bf16), pltpu.VMEM((rows, width), f32)],
        cost_estimate=cost(11_000_000_000, 25_000_000),
        name="feed",
    )(place, block_input, own, other, mixing, mixing_bias, scale, shift, upstream, expand, bias, shrink)


def weight_kernel(images, per, core_ref, *refs):
    lefts, rights = refs[:images], refs[images : 2 * images]
    keep_ref, send_ref, work = refs[2 * images :]
    total = tn_dot(lefts[0][...], rights[0][...])
    for left, right in zip(lefts[1:], rights[1:]):
        total = total + tn_dot(left[...], right[...])
    work[...] = total
    core = core_ref[0]
    share = keep_ref.shape[1]
    for chip in range(per):
        keep_ref[chip] = work[pl.ds(pl.multiple_of((2 * chip + core) * share, 8), share), :]
        send_ref[chip] = work[pl.ds(pl.multiple_of((2 * chip + 1 - core) * share, 8), share), :]


def weight_grad(lefts, rights, core, chips):
    rows, height = lefts[0].shape
    width = rights[0].shape[1]
    share = height // (2 * chips)
    block = max(LANES, 2 * share)
    per = block // (2 * share)
    images = len(lefts)
    tiles = jax.ShapeDtypeStruct((chips, share, width), f32)
    tile_spec = pl.BlockSpec((per, share, width), lambda i, c: (i, 0, 0))
    return pl.pallas_call(
        functools.partial(weight_kernel, images, per),
        grid_spec=pltpu.PrefetchScalarGridSpec(
            num_scalar_prefetch=1,
            grid=(height // block,),
            in_specs=[pl.BlockSpec((rows, block), lambda i, c: (0, i))] * images
            + [pl.BlockSpec((rows, width), lambda i, c: (0, 0))] * images,
            out_specs=[tile_spec, tile_spec],
            scratch_shapes=[pltpu.VMEM((block, width), f32)],
        ),
        out_shape=[tiles, tiles],
        cost_estimate=cost(2 * images * rows * height * width * 3 // 2, 4 * height * width),
        name="weight_grad",
    )(core, *lefts, *rights)


def chip_of(place, chips):
    place = (place + 4 * chips) % chips
    upper = place // (chips // 2)
    return (1 - upper) * 2 * place + upper * (2 * (chips - 1 - place) + 1)

def ring_kernel(chips, count, cuts, *refs):
    keep, sent, out = refs[:count], refs[count:2*count], refs[2*count:3*count]
    other, slot = refs[3*count:4*count], refs[4*count:5*count]
    swap_send, swap_recv, ring_send, ring_recv, pass_send, pass_recv, give_send, give_recv, store = refs[5*count:]
    me = lax.axis_index("dp")
    core, chip = me % 2, me // 2
    column = chip % 2
    place = (1 - column) * (chip // 2) + column * (chips - 1 - chip // 2)
    turn = 1 - 2 * core
    ahead = 2 * chip_of(place + turn, chips) + core
    behind = 2 * chip_of(place - turn, chips) + core
    across = 2 * chip + 1 - core
    barrier = pltpu.get_barrier_semaphore()
    for device in (ahead, behind, across):
        pl.semaphore_signal(barrier, inc=1, device_id={"dp": device}, device_id_type=pl.DeviceIdType.MESH)
    pl.semaphore_wait(barrier, 3)
    def remote(src, dst, send, recv, device):
        return pltpu.make_async_remote_copy(src_ref=src, dst_ref=dst, send_sem=send, recv_sem=recv,
            device_id={"dp": device}, device_id_type=pl.DeviceIdType.MESH)
    def swap_copy(w, s):
        tile = chip_of(place + turn * (s + 1), chips)
        return remote(sent[w].at[tile], other[w].at[tile], swap_send.at[w, s], swap_recv.at[w, s], across)
    def swap_wait(w, s):
        tile = chip_of(place - turn * (s + 1), chips)
        remote(sent[w].at[tile], other[w].at[tile], swap_send.at[w, s], swap_recv.at[w, s], across).wait_recv()
    pieces = [(w, c) for c in range(max(cuts)) for w in range(count) if c < cuts[w]]
    def part(w, c):
        n = slot[w].shape[1] // cuts[w]
        return pl.ds(c * n, n)
    def ring_copy(w, c, s):
        return remote(slot[w].at[s, part(w, c)], slot[w].at[s + 1, part(w, c)],
                      ring_send.at[w, c, s], ring_recv.at[w, c, s], ahead)
    def out_at(w, c, s):
        return out[w].at[chip_of(place - turn * s, chips), core, part(w, c)]
    def start_swap(s, carry):
        for w in range(count):
            swap_copy(w, s).start()
        return carry
    lax.fori_loop(0, chips, start_swap, 0)
    for w in range(count):
        swap_wait(w, 0)
    tile0 = chip_of(place - turn, chips)
    for w, c in pieces:
        slot[w][0, part(w, c)] = keep[w][tile0, part(w, c)] + other[w][tile0, part(w, c)]
        ring_copy(w, c, 0).start()
    def reduce_step(s, carry):
        tile = chip_of(place - turn * (s + 1), chips)
        for w in range(count):
            swap_wait(w, s)
        for w, c in pieces:
            ring_copy(w, c, s - 1).wait_recv()
            slot[w][s, part(w, c)] = slot[w][s, part(w, c)] + (keep[w][tile, part(w, c)] + other[w][tile, part(w, c)])
            @pl.when(s < chips - 1)
            def _():
                ring_copy(w, c, s).start()
            @pl.when(s == chips - 1)
            def _():
                own = slot[w].at[chips - 1, part(w, c)]
                remote(own, out_at(w, c, 0), pass_send.at[w, c, 0], pass_recv.at[w, c, 0], ahead).start()
                remote(own, out_at(w, c, 0), give_send.at[w, c, 0], give_recv.at[w, c, 0], across).start()
                pltpu.make_async_copy(own, out_at(w, c, 0), store.at[w, c]).start()
        return carry
    lax.fori_loop(1, chips, reduce_step, 0)
    def pass_copy(w, c, s):
        return remote(out_at(w, c, s), out_at(w, c, s), pass_send.at[w, c, s], pass_recv.at[w, c, s], ahead)
    def give_copy(w, c, s):
        return remote(out_at(w, c, s), out_at(w, c, s), give_send.at[w, c, s], give_recv.at[w, c, s], across)
    def gather_step(s, carry):
        for w, c in pieces:
            at = out_at(w, c, s)
            remote(at, at, pass_send.at[w, c, s - 1], pass_recv.at[w, c, s - 1], ahead).wait_recv()
            @pl.when(s < chips - 1)
            def _():
                pass_copy(w, c, s).start()
            give_copy(w, c, s).start()
        return carry
    lax.fori_loop(1, chips, gather_step, 0)
    def drain(s, carry):
        for w in range(count):
            swap_copy(w, s).wait_send()
        for w, c in pieces:
            @pl.when(s < chips - 1)
            def _():
                ring_copy(w, c, s).wait_send()
                pass_copy(w, c, s).wait_send()
            give_copy(w, c, s).wait_send()
            theirs = out[w].at[chip_of(place + turn * s, chips), 1 - core, part(w, c)]
            remote(theirs, theirs, give_send.at[w, c, s], give_recv.at[w, c, s], across).wait_recv()
        return carry
    lax.fori_loop(0, chips, drain, 0)
    for w, c in pieces:
        pltpu.make_async_copy(slot[w].at[chips - 1, part(w, c)], out_at(w, c, 0), store.at[w, c]).wait()

def ring_sum(tiles, collective_id, cut=4):
    count = len(tiles)
    chips = tiles[0][0].shape[0]
    cuts = []
    for keep, _ in tiles:
        share = keep.shape[1]
        cuts.append(max(c for c in range(1, cut + 1) if share % (8 * c) == 0))
    hbm = pl.BlockSpec(memory_space=pl.ANY); vmem = pl.BlockSpec(memory_space=pltpu.VMEM)
    dma = lambda *s: pltpu.SemaphoreType.DMA(s)
    most = max(cuts)
    outs = pl.pallas_call(
        functools.partial(ring_kernel, chips, count, tuple(cuts)),
        in_specs=[vmem] * count + [hbm] * count,
        out_specs=[hbm] * count,
        out_shape=[jax.ShapeDtypeStruct((chips, 2) + k.shape[1:], f32) for k, _ in tiles],
        scratch_shapes=[pltpu.VMEM(k.shape, f32) for k, _ in tiles] * 2
        + [dma(count, chips)] * 2 + [dma(count, most, chips)] * 6 + [dma(count, most)],
        compiler_params=pltpu.CompilerParams(collective_id=collective_id, has_side_effects=True),
        name="ring_sum",
    )(*[k for k, _ in tiles], *[s for _, s in tiles])
    return [o.reshape(-1, o.shape[-1]) for o in outs]


def output_kernel(hidden_ref, own_ref, other_ref, bias_ref, *out):
    length = out[-1].shape[0]
    part = pl.ds(0, length)
    out[-1][...] = (
        hidden_ref[part, :] + (own_ref[part, :] + other_ref[part, :]) + bias_ref[...]
    ).astype(bf16)


def input_kernel(grad_ref, own_ref, other_ref, input_ref, scale_ref, *out):
    length = out[-1].shape[0]
    part = pl.ds(0, length)
    normed, inverse = normalize(input_ref[...].astype(f32))
    layer_grad = own_ref[part, :] + other_ref[part, :]
    out[-1][...] = (
        grad_ref[part, :] + norm_back(layer_grad, scale_ref[...], normed, inverse)
    ).astype(bf16)


def finish(kernel, name, image, shape, operands, before):
    images, length, width = shape
    picture = pl.BlockSpec((None, length, width), lambda j: (image, 0, 0))

    def spec(array):
        return picture if array.ndim == 3 else pl.BlockSpec(array.shape, lambda j: (0, 0))

    extra = [] if before is None else [before]
    return pl.pallas_call(
        kernel,
        grid=(1,),
        in_specs=[spec(a) for a in operands] + [pl.BlockSpec(memory_space=pl.ANY)] * len(extra),
        out_specs=picture,
        out_shape=jax.ShapeDtypeStruct(shape, bf16),
        input_output_aliases={len(operands): 0} if extra else {},
        cost_estimate=cost(10_000_000, 10_000_000),
        name=name,
    )(*operands, *extra)


def swap(array):
    return lax.ppermute(array, "tensor", [(0, 1), (1, 0)])


def on_device(
    block_input,
    first_scale,
    first_shift,
    heads_weight,
    heads_bias,
    mixing_weight,
    mixing_bias,
    second_scale,
    second_shift,
    expand_weight,
    expand_bias,
    shrink_weight,
    shrink_bias,
    output_grad,
):
    images, length, width = block_input.shape
    local = heads_weight.shape[2]
    pairs = local // PAIR
    hidden = expand_weight.shape[1]
    rows = -(-length // 16) * 16
    size = lax.axis_size("dp")
    chips = size // 2
    owner = lax.axis_index("tensor")
    core = lax.axis_index("dp") % 2
    cores = [(i, i ^ 1) for i in range(size)]
    place = jnp.stack([owner, core]).astype(jnp.int32)
    which = core.astype(jnp.int32).reshape(1)
    first_scale, first_shift, mixing_bias, second_scale, second_shift, shrink_bias = (
        v.reshape(1, width)
        for v in (first_scale, first_shift, mixing_bias, second_scale, second_shift, shrink_bias)
    )

    half = mixing_weight.shape[0] // 2
    piece = swap(lax.dynamic_slice_in_dim(mixing_weight, core * half, half, 0).astype(f32))
    piece_two = lax.ppermute(piece, "dp", cores)
    full_mixing = gather_weight(place, mixing_weight, piece, piece_two)

    joined = (
        heads_weight.reshape(width, 3, pairs, PAIR).transpose(0, 2, 1, 3).reshape(width, 3 * local)
    )
    zero_bias = jnp.zeros((pairs, PAIR), f32)
    joined_bias = jnp.stack(
        [heads_bias[0].reshape(pairs, PAIR), zero_bias, heads_bias[1].reshape(pairs, PAIR)], axis=1
    ).reshape(1, 3 * local)

    each_image = range(images)
    layer_one, qkv, attended, wide, logsum = zip(
        *[
            attend(i, rows, block_input, joined, joined_bias, first_scale, first_shift)
            for i in each_image
        ]
    )
    hidden_one, layer_two, upstream, activated, pre_low, expand_sums, shrunk, partial_two = zip(
        *[
            feed(
                i, place, block_input, attended[i], swap(wide[i]), full_mixing, mixing_bias,
                second_scale, second_shift, output_grad, expand_weight,
                expand_bias.reshape(1, hidden), shrink_weight,
            )
            for i in each_image
        ]
    )
    shrink_tiles = weight_grad(activated, upstream, which, chips)
    expand_tiles = weight_grad(layer_two, pre_low, which, chips)
    (shrink_full,) = ring_sum([shrink_tiles], 1)

    (
        hidden_grad, hidden_low, stacked, query_bias, value_bias, partial_one, sums_two, sums_one,
    ) = zip(
        *[
            attend_back(
                i, partial_two[i], swap(partial_two[i]), hidden_one[i], upstream[i], mixing_weight,
                qkv[i], logsum[i], joined, block_input, second_scale,
            )
            for i in each_image
        ]
    )
    heads_tiles = weight_grad(layer_one, stacked, which, chips)
    mixing_tiles = weight_grad(attended, hidden_low, which, chips)
    small = jnp.concatenate(
        [
            sum(query_bias).reshape(-1),
            sum(value_bias).reshape(-1),
            sum(expand_sums).reshape(-1),
            sum(sums_two).reshape(-1),
            sum(sums_one).reshape(-1),
        ]
    )
    each = -(-small.shape[0] // size)
    chunk = -(-each // (8 * LANES)) * 8 * LANES
    small_tiles = jnp.pad(small, (0, each * size - small.shape[0])).reshape(size, each)
    small_tiles = jnp.pad(small_tiles, ((0, 0), (0, chunk - each))).reshape(
        chips, 2, chunk // LANES, LANES
    )
    small_pair = (
        lax.dynamic_index_in_dim(small_tiles, core, 1, keepdims=False),
        lax.dynamic_index_in_dim(small_tiles, 1 - core, 1, keepdims=False),
    )
    heads_full, expand_full, mixing_full, small_full = ring_sum(
        [heads_tiles, expand_tiles, mixing_tiles, small_pair], 2
    )
    heads_full = (
        heads_full.reshape(width, pairs, 3, PAIR).transpose(0, 2, 1, 3).reshape(width, 3, local)
    )
    small = small_full.reshape(size, chunk)[:, :each].reshape(-1)

    block_output = input_grad = None
    for i in each_image:
        block_output = finish(
            output_kernel, "output", i, block_input.shape,
            [hidden_one[i], shrunk[i], swap(shrunk[i]), shrink_bias], block_output,
        )
    for i in each_image:
        input_grad = finish(
            input_kernel, "input", i, block_input.shape,
            [hidden_grad[i], partial_one[i], swap(partial_one[i]), block_input, first_scale],
            input_grad,
        )

    parts, at = [], 0
    for count in (2 * local, hidden) + 6 * (width,):
        parts.append(small[at : at + count])
        at += count
    first = jnp.stack(parts[6:8])
    first = first + swap(first)
    return (
        block_output,
        input_grad,
        heads_full,
        parts[0].reshape(2, local),
        mixing_full,
        parts[4],
        parts[2],
        parts[3],
        expand_full,
        parts[1],
        shrink_full,
        parts[5],
        first[0],
        first[1],
    )


def solution(mesh):
    placed = (
        P("dp", None, None),
        P(),
        P(),
        P(None, None, "tensor"),
        P(None, "tensor"),
        P("tensor", None),
        P(),
        P(),
        P(),
        P(None, "tensor"),
        P("tensor"),
        P("tensor", None),
        P(),
        P("dp", None, None),
    )
    return jax.shard_map(
        on_device,
        mesh=mesh,
        in_specs=placed,
        out_specs=(
            P("dp", None, None),
            P("dp", None, None),
            P(None, None, "tensor"),
            P(None, "tensor"),
            P("tensor", None),
            P(),
            P(),
            P(),
            P(None, "tensor"),
            P("tensor"),
            P("tensor", None),
            P(),
            P(),
            P(),
        ),
        check_vma=False,
    )
```

time: 1370 us -> 612 us (0.45)
  waiting for transfers between devices: 829 us -> 43.7 us
  Pallas kernels: 0 us -> 471 us
  matrix products: 216 us -> 0 us
  blocking collectives: 103 us -> 0 us
  local copies, waits for them, and re-layouts: 137 us -> 71.6 us
  other arithmetic: 60.7 us -> 6.32 us
    pallas_call x0 -> x17, Pallas kernels: none -> 471 us  [the longest x2 267 us: ring_sum(): pl.pallas_call(functools.partial(ring_kernel, chips, count, tuple(cuts)),...]
    psum x3 -> x0, waiting for transfers between devices: 425 us -> none  [the longest x1 195 us: on_device(): lax.psum(jnp.dot(activated, shrink_weight, preferred_element_type=jnp.flo...]
    reduce_scatter x4 -> x0, waiting for transfers between devices: 259 us -> none  [the longest x1 108 us: on_device(): lax.psum_scatter(shrink_grad, 'dp', scatter_dimension=0, tiled=True)]
    dot_general x18 -> x0, matrix products: 216 us -> none  [the longest x4 34.7 us: cross_dot(): lax.dot_general(left_side, right_side, (((0,), (0,)), ((), ())), preferre...]
    all_gather x4 -> x0, waiting for transfers between devices: 144 us -> none  [the longest x1 75.1 us: on_device(): lax.all_gather(weight_part[3], 'dp', axis=0, tiled=True)]
    psum x2 -> x0, blocking collectives: 103 us -> none  [the longest x1 61 us: on_device(): lax.psum((heads_bias_grad, expand_bias_grad), 'dp')]
    ppermute x0 -> x11, waiting for transfers between devices: none -> 43.7 us  [the longest x10 43.7 us: swap(): return lax.ppermute(array, 'tensor', [(0, 1), (1, 0)])]
    reduce_sum x9 -> x0, other arithmetic: 41 us -> none  [the longest x1 10.4 us: on_device(): logsum = jax.nn.logsumexp(scores, axis=-1, keepdims=True)]
  transfers between devices with their start and end apart: 11 -> 11, of which waited for: 8 -> 4; matrix products, arithmetic and copies ran while one was open for 15% -> 9% of each run, Pallas kernels for 0% -> 77%
where the time goes in v1:
time: 612 us; the launch traced here: 603 us
  Pallas kernels  471 us (77%)
  local copies, waits for them, and re-layouts  71.6 us (12%)
  waiting for transfers between devices  43.7 us (7%)
  starting transfers between devices  9.4 us (2%)
  other arithmetic  6.32 us (1%)
    pallas_call x2, Pallas kernels, ring_sum(): pl.pallas_call(functools.partial(ring_kernel, chips, count, tuple(cuts)),...  267 us
    pallas_call x2, Pallas kernels, attend_back(): pl.pallas_call(functools.partial(attend_back_kernel, length, chunks, pair...  54.5 us
    pallas_call x2, Pallas kernels, feed(): pl.pallas_call(feed_kernel, grid=(hidden // tile,), in_specs=[pl.BlockSpe...  46.4 us
    ppermute x10, waiting for transfers between devices, swap(): return lax.ppermute(array, 'tensor', [(0, 1), (1, 0)])  43.7 us
    pallas_call x4, Pallas kernels, weight_grad(): pl.pallas_call(functools.partial(weight_kernel, images, per), grid_spec=p...  42.6 us
    unnamed x42, local copies, waits for them, and re-layouts  42 us
    pallas_call x2, Pallas kernels, attend(): pl.pallas_call(functools.partial(attend_kernel, length, chunks), grid=(pa...  36 us
    pallas_call x4, Pallas kernels, finish(): pl.pallas_call(kernel, grid=(1,), in_specs=[spec(a) for a in operands] +...  21.1 us
  transfers between devices with their start and end apart: 11, of which 4 were waited for; matrix products, arithmetic and copies ran while one was open for 9% of the time, Pallas kernels for 77%

profile of v1, /device:TPU:0, one launch (start us, length us, event | category | flops | bytes accessed | tf_op | source)
XLA Modules:
  0.0 603.3 jit_solution(6959667605585955068)
XLA Ops:
  0.7 2.1 dynamic-slice_convert_fusion
  2.8 3.0 collective-permute-start.1
  5.8 3.8 copy.70.input_ref
  9.6 3.0 copy.64
  12.6 2.4 copy.65
  15.1 2.9 copy.69.weight_ref.joined_ref
  18.2 0.6 reshape.101.bias_ref
  18.8 17.9 %attend.2 = (bf16[592,1024]{1,0:T(8,128)(2,1)}, bf16[592,1536]{1,0:T(8,128)(2,1)}, bf16[592,512]{1,0:T(8,128)(2,1)}, f32[592,512]{1,0:T(8,128)}, f32[4,5,1,256]{3,2,1,0:T(1,128)}) custom-call(bf16[2,577,1024]{2,1,0:T(8,128)(2,1)} %copy.70.input_ref, bf16[1024,1536]{1,0:T(8,128)(2,1)} %copy.69.weight_ref.joined_ref, f32[1,1536]{1,0:T(1,128)} %reshape.101.bias_ref, ...), custom_call_target="tpu_custom_call" | custom-call | flops 10000000000 | bytes 10000000 | tf_op jit(solution)/shard_map/attend/pallas_call | solution.py:124
  36.9 18.1 %attend.3 = (bf16[592,1024]{1,0:T(8,128)(2,1)}, bf16[592,1536]{1,0:T(8,128)(2,1)}, bf16[592,512]{1,0:T(8,128)(2,1)}, f32[592,512]{1,0:T(8,128)}, f32[4,5,1,256]{3,2,1,0:T(1,128)}) custom-call(bf16[2,577,1024]{2,1,0:T(8,128)(2,1)} %copy.70.input_ref, bf16[1024,1536]{1,0:T(8,128)(2,1)} %copy.69.weight_ref.joined_ref, f32[1,1536]{1,0:T(1,128)} %reshape.101.bias_ref, ...), custom_call_target="tpu_custom_call" | custom-call | flops 10000000000 | bytes 10000000 | tf_op jit(solution)/shard_map/attend/pallas_call | solution.py:124
  55.1 1.8 collective-permute-start.4
  56.8 2.1 copy.71.upstream_ref
  59.6 1.0 copy-done.4
  60.6 3.4 gather_weight.1.mixing_ref
  63.9 2.7 collective-permute-done.other_ref
  66.6 23.3 %feed.2 = (f32[592,1024]{1,0:T(8,128)}, bf16[592,1024]{1,0:T(8,128)(2,1)}, bf16[592,1024]{1,0:T(8,128)(2,1)}, bf16[592,2048]{1,0:T(8,128)(2,1)}, bf16[592,2048]{...) custom-call(s32[2]{0:T(128)} %pad_add_fusion.place_ref, ...), custom_call_target="tpu_custom_call" | custom-call | flops 11000000512 | bytes 25000000 | tf_op jit(solution)/shard_map/feed/pallas_call | solution.py:368
  90.2 1.8 collective-permute-done.4.other_ref
  92.0 23.1 %feed.3 = (f32[592,1024]{1,0:T(8,128)}, bf16[592,1024]{1,0:T(8,128)(2,1)}, bf16[592,1024]{1,0:T(8,128)(2,1)}, bf16[592,2048]{1,0:T(8,128)(2,1)}, bf16[592,2048]{...) custom-call(s32[2]{0:T(128)} %pad_add_fusion.place_ref, ...), custom_call_target="tpu_custom_call" | custom-call | flops 11000000512 | bytes 25000000 | tf_op jit(solution)/shard_map/feed/pallas_call | solution.py:368
  115.5 1.7 collective-permute-start.3
  117.6 0.7 add.39
  118.3 13.0 %weight_grad.5 = (f32[8,64,2048]{2,1,0:T(8,128)}, f32[8,64,2048]{2,1,0:T(8,128)}) custom-call(s32[1]{0:T(128)} %bitcast.1.core_ref, bf16[592,1024]{1,0:T(8,128)(2,1)} %get-tuple-element.93.refs_0_, bf16[592,1024]{1,0:T(8,128)(2,1)} %get-tuple-element.94.refs_1_, bf16[592,2048]{1,0:T(8,128)(2,1)} %get-tuple-element.95.refs_2_, ...), custom_call_target="tpu_custom_call" | custom-call | flops 7449083904 | bytes 8388608 | tf_op jit(solution)/shard_map/weight_grad/pallas_call | solution.py:425
  131.3 14.5 %collective-permute-done.6.other_ref = f32[592,1024]{1,0:T(8,128)} collective-permute-done((f32[592,1024]{1,0:T(8,128)}, f32[592,1024]{1,0:T(8,128)}, u32[]{:S(2)}, u32[]{:S(2)}) %collective-permute-start.6) | collective-permute-done | bytes 2424864 | tf_op jit(solution)/shard_map/ppermute | solution.py:601
  145.9 27.1 %attend_back.2 = (f32[592,1024]{1,0:T(8,128)}, bf16[592,1024]{1,0:T(8,128)(2,1)}, bf16[592,1536]{1,0:T(8,128)(2,1)}, f32[1,512]{1,0:T(1,128)}, f32[1,512]{1,0:T(...) custom-call(f32[592,1024]{1,0:T(8,128)} %get-tuple-element.76.own_ref, ...), custom_call_target="tpu_custom_call" | custom-call | flops 12000000000 | bytes 20000000 | tf_op jit(solution)/shard_map/attend_back/pallas_call | solution.py:232
  173.2 24.6 %collective-permute-done.8.other_ref = f32[592,1024]{1,0:T(8,128)} collective-permute-done((f32[592,1024]{1,0:T(8,128)}, f32[592,1024]{1,0:T(8,128)}, u32[]{:S(2)}, u32[]{:S(2)}) %collective-permute-start.8) | collective-permute-done | bytes 2424864 | tf_op jit(solution)/shard_map/ppermute | solution.py:601
  197.8 27.3 %attend_back.3 = (f32[592,1024]{1,0:T(8,128)}, bf16[592,1024]{1,0:T(8,128)(2,1)}, bf16[592,1536]{1,0:T(8,128)(2,1)}, f32[1,512]{1,0:T(1,128)}, f32[1,512]{1,0:T(...) custom-call(f32[592,1024]{1,0:T(8,128)} %get-tuple-element.82.own_ref, ...), custom_call_target="tpu_custom_call" | custom-call | flops 12000000000 | bytes 20000000 | tf_op jit(solution)/shard_map/attend_back/pallas_call | solution.py:232
  225.4 0.7 add.37
  226.1 0.7 add.38
  226.8 0.7 add_bitcast_fusion
  227.5 0.7 add_bitcast_fusion.1
  228.3 0.6 dynamic-slice_bitcast_fusion
  228.9 5.8 weight_grad.6
  234.7 11.3 %weight_grad.4 = (f32[8,64,1536]{2,1,0:T(8,128)}, f32[8,64,1536]{2,1,0:T(8,128)}) custom-call(s32[1]{0:T(128)} %bitcast.1.core_ref, bf16[592,1024]{1,0:T(8,128)(2,1)} %get-tuple-element.88.refs_0_, bf16[592,1024]{1,0:T(8,128)(2,1)} %get-tuple-element.89.refs_1_, bf16[592,1536]{1,0:T(8,128)(2,1)} %get-tuple-element.90.refs_2_, ...), custom_call_target="tpu_custom_call" | custom-call | flops 5586812928 | bytes 6291456 | tf_op jit(solution)/shard_map/weight_grad/pallas_call | solution.py:425
  246.0 177.3 %ring_sum.2 = (f32[8,2,64,1536]{3,2,1,0:T(8,128)}, f32[8,2,64,2048]{3,2,1,0:T(8,128)}, f32[8,2,32,1024]{3,2,1,0:T(8,128)}, f32[8,2,8,128]{3,2,1,0:T(8,128)}) custom-call(f32[8,64,1536]{2,1,0:T(8,128)} %get-tuple-element.92.refs_0_, f32[8,64,2048]{2,1,0:T(8,128)} %get-tuple-element.97.refs_1_, f32[8,32,1024]{2,1,0:T(8,128)} %get-tuple-element.100.refs_2_, ...), custom_call_target="tpu_custom_call" | custom-call | tf_op jit(solution)/shard_map/ring_sum/pallas_call | solution.py:549
  423.3 0.9 copy.93
  424.9 1.4 collective-permute-start.10
  426.3 12.5 %weight_grad.7 = (f32[8,128,1024]{2,1,0:T(8,128)}, f32[8,128,1024]{2,1,0:T(8,128)}) custom-call(s32[1]{0:T(128)} %bitcast.1.core_ref, bf16[592,2048]{1,0:T(8,128)(2,1)} %get-tuple-element.118.refs_0_, bf16[592,2048]{1,0:T(8,128)(2,1)} %get-tuple-element.119.refs_1_, bf16[592,1024]{1,0:T(8,128)(2,1)} %get-tuple-element.83.upstream_ref.refs_2_, ...), custom_call_target="tpu_custom_call" | custom-call | flops 7449083904 | bytes 8388608 | tf_op jit(solution)/shard_map/weight_grad/pallas_call | solution.py:425
  438.8 89.9 %ring_sum.3 = f32[8,2,128,1024]{3,2,1,0:T(8,128)} custom-call(f32[8,128,1024]{2,1,0:T(8,128)} %get-tuple-element.120.refs_0_, f32[8,128,1024]{2,1,0:T(8,128)} %get-tuple-element.121.refs_1_), custom_call_target="tpu_custom_call" | custom-call | tf_op jit(solution)/shard_map/ring_sum/pallas_call | solution.py:549
  529.4 4.5 output.2.out_0_
  533.9 4.5 output.3
  538.4 5.5 copy.83
  543.9 11.3 %reshape_reshape.6 = f32[1024,4,3,128]{3,2,1,0:T(4,128)} reshape(f32[8,2,64,1536]{3,2,1,0:T(8,128)} %get-tuple-element.114) | data formatting | bytes 12582912 | tf_op jit(solution)/shard_map/reshape;reshape | solution.py:707
  555.2 9.0 %copy.82 = f32[1024,3,4,128]{0,3,2,1:T(8,128)} copy(f32[1024,3,4,128]{3,1,2,0:T(4,128)} %bitcast.57) | data formatting | bytes 12582912 | tf_op jit(solution)/shard_map/transpose | solution.py:707
  564.2 6.6 %copy.85 = f32[1024,3,512]{2,0,1:T(8,128)} copy(f32[1024,3,512]{0,2,1:T(8,128)} %bitcast.61) | data formatting | bytes 12582912
  572.0 6.1 %input.2.out_0_ = bf16[2,577,1024]{2,1,0:T(8,128)(2,1)} custom-call(f32[592,1024]{1,0:T(8,128)} %get-tuple-element.86.grad_ref, f32[592,1024]{1,0:T(8,128)} %get-tuple-element.87.own_ref, f32[592,1024]{1,0:T(8,128)} %collective-permute-done.9.other_ref, bf16[2,577,1024]{2,1,0:T(8,128)(2,1)} %copy.70.input_ref, f32[1,1024]{1,0:T(1,128)} %bitcast.78), custom_call_target="tpu_custom_call" | custom-call | flops 10000000 | bytes 10000000 | tf_op jit(solution)/shard_map/input/pallas_call | solution.py:588
  578.1 6.1 %input.3 = bf16[2,577,1024]{2,1,0:T(8,128)(2,1)} custom-call(f32[592,1024]{1,0:T(8,128)} %get-tuple-element.80.grad_ref, f32[592,1024]{1,0:T(8,128)} %get-tuple-element.81.own_ref, f32[592,1024]{1,0:T(8,128)} %collective-permute-done.7.other_ref, bf16[2,577,1024]{2,1,0:T(8,128)(2,1)} %copy.70.input_ref, ...), custom_call_target="tpu_custom_call", output_to_operand_aliasing={{}: (5, {})} | custom-call | flops 10000000 | bytes 10000000 | tf_op jit(solution)/shard_map/input/pallas_call | solution.py:588
  584.1 5.7 copy.84
  589.8 1.3 copy.104
  591.1 8.6 %copy.105 = f32[1024,2048]{1,0:T(8,128)} copy(f32[1024,2048]{1,0:T(8,128)} %bitcast.64) | data formatting | bytes 16777216
  599.7 3.4 copy.106
  (62 shorter events, 5.1 us)
Async XLA Ops:
  2.8 6.8 %copy-start = (bf16[1024,3,512]{2,0,1:T(8,128)(2,1)S(1)}, bf16[1024,3,512]{2,0,1:T(8,128)(2,1)}, u32[]{:S(2)}) copy-start(bf16[1024,3,512]{2,0,1:T(8,128)(2,1)} %param.17) | copy-start | bytes 9437188
  2.8 34.1 %collective-permute-start.1 = (f32[256,1024]{1,0:T(8,128)}, f32[256,1024]{1,0:T(8,128)}, u32[]{:S(2)}, u32[]{:S(2)}) collective-permute-start(f32[256,1024]{1,0:T(8,128)} %dynamic-slice_convert_fusion), channel_id=1, source_target_pairs={{0,1},{1,0},{2,3},{3,2},{4,5},{5,4},{6,7},{7,6},{8,9},{9,8},{10,11... | collective-permute-start | bytes 3145736 | tf_op jit(solution)/shard_map/ppermute | solution.py:601
  15.1 2.9 copy-start.8
  36.7 20.1 %copy-start.2 = (bf16[2,577,1024]{2,0,1:T(2,128)(2,1)S(1)}, bf16[2,577,1024]{2,0,1:T(2,128)(2,1)}, u32[]{:S(2)}) copy-start(bf16[2,577,1024]{2,0,1:T(2,128)(2,1)} %param.27) | copy-start | bytes 7090180
  36.7 29.9 %collective-permute-start = (f32[592,512]{1,0:T(8,128)}, f32[592,512]{1,0:T(8,128)}, u32[]{:S(2)}, u32[]{:S(2)}) collective-permute-start(f32[592,512]{1,0:T(8,128)} %get-tuple-element.69), channel_id=1, source_target_pairs={{0,1},{1,0},{2,3},{3,2},{4,5},{5,4},{6,7},{7,6},{8,9},{9,8},{10,11... | collective-permute-start | bytes 3637256 | tf_op jit(solution)/shard_map/ppermute | solution.py:601
  36.9 22.6 %collective-permute-start.2 = (f32[256,1024]{1,0:T(8,128)}, f32[256,1024]{1,0:T(8,128)S(1)}, u32[]{:S(2)}, u32[]{:S(2)}) collective-permute-start(f32[256,1024]{1,0:T(8,128)} %collective-permute-done.1.near_ref), channel_id=1, source_target_pairs={{0,2},{2,0},{4,6},{6,4},{8,10},{10,8},{12,14},{14,12},{16,18},{18,... | collective-permute-start | bytes 3145736 | tf_op jit(solution)/shard_map/ppermute | solution.py:639
  55.1 36.9 %collective-permute-start.4 = (f32[592,512]{1,0:T(8,128)}, f32[592,512]{1,0:T(8,128)}, u32[]{:S(2)}, u32[]{:S(2)}) collective-permute-start(f32[592,512]{1,0:T(8,128)} %get-tuple-element.73), channel_id=1, source_target_pairs={{0,1},{1,0},{2,3},{3,2},{4,5},{5,4},{6,7},{7,6},{8,9},{9,8},{10,11... | collective-permute-start | bytes 3637256 | tf_op jit(solution)/shard_map/ppermute | solution.py:601
  59.5 1.0 copy-start.4
  90.0 55.9 %collective-permute-start.6 = (f32[592,1024]{1,0:T(8,128)}, f32[592,1024]{1,0:T(8,128)}, u32[]{:S(2)}, u32[]{:S(2)}) collective-permute-start(f32[592,1024]{1,0:T(8,128)} %get-tuple-element.76.own_ref), channel_id=1, source_target_pairs={{0,1},{1,0},{2,3},{3,2},{4,5},{5,4},{6,7},{7,6},{8,9},{9,8},{10,11... | collective-permute-start | bytes 7274504 | tf_op jit(solution)/shard_map/ppermute | solution.py:601
  92.0 23.5 %copy-start.1 = (f32[592,1024]{1,0:T(8,128)S(1)}, f32[592,1024]{1,0:T(8,128)}, u32[]{:S(2)}) copy-start(f32[592,1024]{1,0:T(8,128)} %get-tuple-element.71.own_ref) | copy-start | bytes 7274500
  92.0 25.6 %copy-start.6 = (f32[1,2048]{1,0:T(1,128)S(1)}, f32[1,2048]{1,0:T(1,128)}, u32[]{:S(2)}) copy-start(f32[1,2048]{1,0:T(1,128)} %get-tuple-element.106) | copy-start | bytes 24580
  115.1 82.7 %collective-permute-start.8 = (f32[592,1024]{1,0:T(8,128)}, f32[592,1024]{1,0:T(8,128)}, u32[]{:S(2)}, u32[]{:S(2)}) collective-permute-start(f32[592,1024]{1,0:T(8,128)} %get-tuple-element.82.own_ref), channel_id=1, source_target_pairs={{0,1},{1,0},{2,3},{3,2},{4,5},{5,4},{6,7},{7,6},{8,9},{9,8},{10,11... | collective-permute-start | bytes 7274504 | tf_op jit(solution)/shard_map/ppermute | solution.py:601
  115.5 418.4 %collective-permute-start.3 = (f32[592,1024]{1,0:T(8,128)S(1)}, f32[592,1024]{1,0:T(8,128)}, u32[]{:S(2)}, u32[]{:S(2)}) collective-permute-start(f32[592,1024]{1,0:T(8,128)S(1)} %copy-done.1), channel_id=1, source_target_pairs={{0,1},{1,0},{2,3},{3,2},{4,5},{5,4},{6,7},{7,6},{8,9},{9,8},{10,11... | collective-permute-start | bytes 7274504 | tf_op jit(solution)/shard_map/ppermute | solution.py:601
  117.2 412.2 %collective-permute-start.5 = (f32[592,1024]{1,0:T(8,128)}, f32[592,1024]{1,0:T(8,128)}, u32[]{:S(2)}, u32[]{:S(2)}) collective-permute-start(f32[592,1024]{1,0:T(8,128)} %get-tuple-element.75.own_ref), channel_id=1, source_target_pairs={{0,1},{1,0},{2,3},{3,2},{4,5},{5,4},{6,7},{7,6},{8,9},{9,8},{10,11... | collective-permute-start | bytes 7274504 | tf_op jit(solution)/shard_map/ppermute | solution.py:601
  173.0 405.1 %collective-permute-start.7 = (f32[592,1024]{1,0:T(8,128)}, f32[592,1024]{1,0:T(8,128)}, u32[]{:S(2)}, u32[]{:S(2)}) collective-permute-start(f32[592,1024]{1,0:T(8,128)} %get-tuple-element.81.own_ref), channel_id=1, source_target_pairs={{0,1},{1,0},{2,3},{3,2},{4,5},{5,4},{6,7},{7,6},{8,9},{9,8},{10,11... | collective-permute-start | bytes 7274504 | tf_op jit(solution)/shard_map/ppermute | solution.py:601
  197.8 27.5 %copy-start.10 = (f32[1,512]{1,0:T(1,128)S(1)}, f32[1,512]{1,0:T(1,128)}, u32[]{:S(2)}) copy-start(f32[1,512]{1,0:T(1,128)} %get-tuple-element.102) | copy-start | bytes 6148
  197.8 28.2 %copy-start.9 = (f32[1,512]{1,0:T(1,128)S(1)}, f32[1,512]{1,0:T(1,128)}, u32[]{:S(2)}) copy-start(f32[1,512]{1,0:T(1,128)} %get-tuple-element.104) | copy-start | bytes 6148
  197.8 28.9 %copy-start.5 = (f32[4,1024]{1,0:T(4,128)S(1)}, f32[4,1024]{1,0:T(4,128)}, u32[]{:S(2)}) copy-start(f32[4,1024]{1,0:T(4,128)} %get-tuple-element.108) | copy-start | bytes 49156
  197.8 29.7 %copy-start.7 = (f32[2,1024]{1,0:T(2,128)S(1)}, f32[2,1024]{1,0:T(2,128)}, u32[]{:S(2)}) copy-start(f32[2,1024]{1,0:T(2,128)} %get-tuple-element.110) | copy-start | bytes 24580
  225.2 346.8 %collective-permute-start.9 = (f32[592,1024]{1,0:T(8,128)}, f32[592,1024]{1,0:T(8,128)}, u32[]{:S(2)}, u32[]{:S(2)}) collective-permute-start(f32[592,1024]{1,0:T(8,128)} %get-tuple-element.87.own_ref), channel_id=1, source_target_pairs={{0,1},{1,0},{2,3},{3,2},{4,5},{5,4},{6,7},{7,6},{8,9},{9,8},{10,11... | collective-permute-start | bytes 7274504 | tf_op jit(solution)/shard_map/ppermute | solution.py:601
  424.9 146.5 %collective-permute-start.10 = (f32[2,1024]{1,0:T(2,128)S(1)}, f32[2,1024]{1,0:T(2,128)S(1)}, u32[]{:S(2)}, u32[]{:S(2)}) collective-permute-start(f32[2,1024]{1,0:T(2,128)S(1)} %pad_maximum_fusion.1), channel_id=1, source_target_pairs={{0,1},{1,0},{2,3},{3,2},{4,5},{5,4},{6,7},{7,6},{8,9},{9,8},{10,11... | collective-permute-start | bytes 24584 | tf_op jit(solution)/shard_map/ppermute | solution.py:601
  584.1 5.7 copy-start.3
  589.8 9.9 %slice-start = ((s8[8388608]{0:T(1024)(128)(4,1)}), s8[4194304]{0:T(1024)(128)(4,1)S(1)}, s32[]{:S(2)}) async-start(s8[8388608]{0:T(1024)(128)(4,1)} %bitcast.58), calls=%async_computation | async-start | bytes 8388608
  591.1 8.6 %slice-start.1 = ((s8[8388608]{0:T(1024)(128)(4,1)}), s8[4194304]{0:T(1024)(128)(4,1)S(1)}, s32[]{:S(2)}) async-start(s8[8388608]{0:T(1024)(128)(4,1)} %bitcast.58), calls=%async_computation.1 | async-start | bytes 8388608

commit v2 on v1

--- a/solution.py
+++ b/solution.py
@@ -7,6 +7,7 @@
 from jax.experimental import pallas as pl
 from jax.experimental.pallas import tpu as pltpu
 from jax.sharding import PartitionSpec as P
+
 
 HEAD_DIM = 64
 PAIR = 2 * HEAD_DIM
@@ -159,7 +160,7 @@
     length, chunks, pairs, own_ref, other_ref, hidden_ref, upstream_ref, mixing_ref, qkv_ref,
     logsum_ref, joined_ref, input_ref, scale_ref,
     grad_ref, low_ref, out_ref, qbias_ref, vbias_ref, partial_ref, sums_ref, first_ref,
-    block, queries, grads, query_out, key_sum, value_sum, stacked_all,
+    block, queries, grads, query_out, key_sum, value_sum, stacked_all, mark=None,
 ):
     pair = pl.program_id(0)
     rows = qkv_ref.shape[0]
@@ -188,7 +189,9 @@
     value_sum[...] = jnp.zeros_like(value_sum)
 
     def body(step, bias):
-        at = pl.ds(pl.multiple_of(step * QUERIES, QUERIES), QUERIES)
+        if mark is not None:
+            mark(step)
+        at = pl.ds(step * QUERIES, QUERIES)
         stacked = stack_heads(queries[at, :], factor)
         upstream = stack_heads(grads[at, :], 1.0)
         probs = jnp.exp(nt_dot(keys, stacked) - logsum_ref[step])
@@ -202,7 +205,10 @@
         query_out[at, :] = query_grad.astype(bf16)
         return bias + jnp.sum(query_grad, axis=0, keepdims=True)
 
-    qbias_ref[...] = lax.fori_loop(0, chunks, body, jnp.zeros((1, PAIR), f32), unroll=True)
+    bias = jnp.zeros((1, PAIR), f32)
+    for step in range(chunks):
+        bias = body(step, bias)
+    qbias_ref[...] = bias
     wide = jnp.zeros((rows, PAIR), f32)
     value_grad = jnp.where(keep, value_sum[...], wide)
     vbias_ref[...] = jnp.sum(value_grad, axis=0, keepdims=True)
@@ -221,56 +227,71 @@
         first_ref[1:2, :] = jnp.sum(partial, axis=0, keepdims=True)
 
 
-def attend_back(image, own, other, hidden, upstream, mixing, qkv, logsum, joined, block_input, scale):
+def attend_back(
+    image, own, other, hidden, upstream, mixing, qkv, logsum, joined, block_input, scale,
+    own_tile, chips, collective_id,
+):
     rows, width = own.shape
     length = block_input.shape[1]
     pairs = joined.shape[1] // (3 * PAIR)
     chunks = -(-rows // QUERIES)
-    full = pl.BlockSpec((rows, width), lambda j: (0, 0))
+    once = dict(pipeline_mode=pl.Buffered(1))
+    full = pl.BlockSpec((rows, width), lambda j: (0, 0), **once)
+    out = pl.BlockSpec((rows, width), lambda j: (0, 0))
     stack = pl.BlockSpec((rows, 3 * PAIR), lambda j: (0, j))
     bias = pl.BlockSpec((1, PAIR), lambda j: (0, j))
-    return pl.pallas_call(
-        functools.partial(attend_back_kernel, length, chunks, pairs),
-        grid=(pairs,),
-        in_specs=[
-            full,
-            full,
-            full,
-            full,
-            pl.BlockSpec((PAIR, width), lambda j: (j, 0)),
-            stack,
-            pl.BlockSpec((None, chunks, 1, 2 * QUERIES), lambda j: (j, 0, 0, 0)),
-            pl.BlockSpec(joined.shape, lambda j: (0, 0)),
-            pl.BlockSpec((None, length, width), lambda j: (image, 0, 0)),
-            pl.BlockSpec((1, width), lambda j: (0, 0)),
-        ],
-        out_specs=[
-            full,
-            full,
-            stack,
-            bias,
-            bias,
-            full,
-            pl.BlockSpec((4, width), lambda j: (0, 0)),
-            pl.BlockSpec((2, width), lambda j: (0, 0)),
-        ],
-        out_shape=[
-            jax.ShapeDtypeStruct((rows, width), f32),
-            jax.ShapeDtypeStruct((rows, width), bf16),
-            jax.ShapeDtypeStruct((rows, pairs * 3 * PAIR), bf16),
-            jax.ShapeDtypeStruct((1, pairs * PAIR), f32),
-            jax.ShapeDtypeStruct((1, pairs * PAIR), f32),
-            jax.ShapeDtypeStruct((rows, width), f32),
-            jax.ShapeDtypeStruct((4, width), f32),
-            jax.ShapeDtypeStruct((2, width), f32),
-        ],
-        scratch_shapes=[pltpu.VMEM((rows, width), f32)]
+    in_specs = [
+        full,
+        full,
+        full,
+        full,
+        pl.BlockSpec((PAIR, width), lambda j: (j, 0)),
+        stack,
+        pl.BlockSpec((None, chunks, 1, 2 * QUERIES), lambda j: (j, 0, 0, 0)),
+        pl.BlockSpec(joined.shape, lambda j: (0, 0), **once),
+        pl.BlockSpec((None, length, width), lambda j: (image, 0, 0), **once),
+        pl.BlockSpec((1, width), lambda j: (0, 0)),
+    ]
+    out_specs = [
+        out,
+        out,
+        stack,
+        bias,
+        bias,
+        out,
+        pl.BlockSpec((4, width), lambda j: (0, 0)),
+        pl.BlockSpec((2, width), lambda j: (0, 0)),
+    ]
+    out_shape = [
+        jax.ShapeDtypeStruct((rows, width), f32),
+        jax.ShapeDtypeStruct((rows, width), bf16),
+        jax.ShapeDtypeStruct((rows, pairs * 3 * PAIR), bf16),
+        jax.ShapeDtypeStruct((1, pairs * PAIR), f32),
+        jax.ShapeDtypeStruct((1, pairs * PAIR), f32),
+        jax.ShapeDtypeStruct((rows, width), f32),
+        jax.ShapeDtypeStruct((4, width), f32),
+        jax.ShapeDtypeStruct((2, width), f32),
+    ]
+    scratch = (
+        [pltpu.VMEM((rows, width), f32)]
         + [pltpu.VMEM((chunks * QUERIES, PAIR), bf16)] * 3
         + [pltpu.VMEM((rows, PAIR), f32)] * 2
-        + [pltpu.VMEM((rows, pairs * 3 * PAIR), bf16)],
-        cost_estimate=cost(12_000_000_000, 20_000_000),
+        + [pltpu.VMEM((rows, pairs * 3 * PAIR), bf16)]
+    )
+    operands = [own, other, hidden, upstream, mixing, qkv, logsum, joined, block_input, scale]
+    ins, outs, shapes, extra = Gather.specs(own_tile, chips)
+    kernel = functools.partial(attend_back_kernel, length, chunks, pairs)
+    return pl.pallas_call(
+        riding(kernel, len(in_specs), len(out_specs), len(scratch), pairs, chunks),
+        grid=(pairs,),
+        in_specs=in_specs + ins,
+        out_specs=out_specs + outs,
+        out_shape=out_shape + shapes,
+        scratch_shapes=scratch + extra,
+        compiler_params=pltpu.CompilerParams(collective_id=collective_id, has_side_effects=True),
+        cost_estimate=cost(40_000_000_000, 20_000_000),
         name="attend_back",
-    )(own, other, hidden, upstream, mixing, qkv, logsum, joined, block_input, scale)
+    )(*operands, own_tile)
 
 
 def gather_kernel(place_ref, own_ref, near_ref, far_ref, out_ref):
@@ -399,164 +420,417 @@
     )(place, block_input, own, other, mixing, mixing_bias, scale, shift, upstream, expand, bias, shrink)
 
 
-def weight_kernel(images, per, core_ref, *refs):
-    lefts, rights = refs[:images], refs[images : 2 * images]
-    keep_ref, send_ref, work = refs[2 * images :]
-    total = tn_dot(lefts[0][...], rights[0][...])
-    for left, right in zip(lefts[1:], rights[1:]):
-        total = total + tn_dot(left[...], right[...])
-    work[...] = total
-    core = core_ref[0]
-    share = keep_ref.shape[1]
-    for chip in range(per):
-        keep_ref[chip] = work[pl.ds(pl.multiple_of((2 * chip + core) * share, 8), share), :]
-        send_ref[chip] = work[pl.ds(pl.multiple_of((2 * chip + 1 - core) * share, 8), share), :]
-
-
-def weight_grad(lefts, rights, core, chips):
-    rows, height = lefts[0].shape
-    width = rights[0].shape[1]
-    share = height // (2 * chips)
-    block = max(LANES, 2 * share)
-    per = block // (2 * share)
-    images = len(lefts)
-    tiles = jax.ShapeDtypeStruct((chips, share, width), f32)
-    tile_spec = pl.BlockSpec((per, share, width), lambda i, c: (i, 0, 0))
-    return pl.pallas_call(
-        functools.partial(weight_kernel, images, per),
-        grid_spec=pltpu.PrefetchScalarGridSpec(
-            num_scalar_prefetch=1,
-            grid=(height // block,),
-            in_specs=[pl.BlockSpec((rows, block), lambda i, c: (0, i))] * images
-            + [pl.BlockSpec((rows, width), lambda i, c: (0, 0))] * images,
-            out_specs=[tile_spec, tile_spec],
-            scratch_shapes=[pltpu.VMEM((block, width), f32)],
-        ),
-        out_shape=[tiles, tiles],
-        cost_estimate=cost(2 * images * rows * height * width * 3 // 2, 4 * height * width),
-        name="weight_grad",
-    )(core, *lefts, *rights)
-
-
 def chip_of(place, chips):
     place = (place + 4 * chips) % chips
     upper = place // (chips // 2)
     return (1 - upper) * 2 * place + upper * (2 * (chips - 1 - place) + 1)
 
-def ring_kernel(chips, count, cuts, *refs):
-    keep, sent, out = refs[:count], refs[count:2*count], refs[2*count:3*count]
-    other, slot = refs[3*count:4*count], refs[4*count:5*count]
-    swap_send, swap_recv, ring_send, ring_recv, pass_send, pass_recv, give_send, give_recv, store = refs[5*count:]
-    me = lax.axis_index("dp")
-    core, chip = me % 2, me // 2
-    column = chip % 2
-    place = (1 - column) * (chip // 2) + column * (chips - 1 - chip // 2)
-    turn = 1 - 2 * core
-    ahead = 2 * chip_of(place + turn, chips) + core
-    behind = 2 * chip_of(place - turn, chips) + core
-    across = 2 * chip + 1 - core
-    barrier = pltpu.get_barrier_semaphore()
-    for device in (ahead, behind, across):
-        pl.semaphore_signal(barrier, inc=1, device_id={"dp": device}, device_id_type=pl.DeviceIdType.MESH)
-    pl.semaphore_wait(barrier, 3)
-    def remote(src, dst, send, recv, device):
-        return pltpu.make_async_remote_copy(src_ref=src, dst_ref=dst, send_sem=send, recv_sem=recv,
-            device_id={"dp": device}, device_id_type=pl.DeviceIdType.MESH)
-    def swap_copy(w, s):
-        tile = chip_of(place + turn * (s + 1), chips)
-        return remote(sent[w].at[tile], other[w].at[tile], swap_send.at[w, s], swap_recv.at[w, s], across)
-    def swap_wait(w, s):
-        tile = chip_of(place - turn * (s + 1), chips)
-        remote(sent[w].at[tile], other[w].at[tile], swap_send.at[w, s], swap_recv.at[w, s], across).wait_recv()
-    pieces = [(w, c) for c in range(max(cuts)) for w in range(count) if c < cuts[w]]
-    def part(w, c):
-        n = slot[w].shape[1] // cuts[w]
-        return pl.ds(c * n, n)
-    def ring_copy(w, c, s):
-        return remote(slot[w].at[s, part(w, c)], slot[w].at[s + 1, part(w, c)],
-                      ring_send.at[w, c, s], ring_recv.at[w, c, s], ahead)
-    def out_at(w, c, s):
-        return out[w].at[chip_of(place - turn * s, chips), core, part(w, c)]
-    def start_swap(s, carry):
-        for w in range(count):
-            swap_copy(w, s).start()
-        return carry
-    lax.fori_loop(0, chips, start_swap, 0)
-    for w in range(count):
-        swap_wait(w, 0)
-    tile0 = chip_of(place - turn, chips)
-    for w, c in pieces:
-        slot[w][0, part(w, c)] = keep[w][tile0, part(w, c)] + other[w][tile0, part(w, c)]
-        ring_copy(w, c, 0).start()
-    def reduce_step(s, carry):
-        tile = chip_of(place - turn * (s + 1), chips)
-        for w in range(count):
-            swap_wait(w, s)
-        for w, c in pieces:
-            ring_copy(w, c, s - 1).wait_recv()
-            slot[w][s, part(w, c)] = slot[w][s, part(w, c)] + (keep[w][tile, part(w, c)] + other[w][tile, part(w, c)])
-            @pl.when(s < chips - 1)
+
+def remote(source, target, send, receive, device):
+    return pltpu.make_async_remote_copy(
+        src_ref=source,
+        dst_ref=target,
+        send_sem=send,
+        recv_sem=receive,
+        device_id={"dp": device},
+        device_id_type=pl.DeviceIdType.MESH,
+    )
+
+
+class Place:
+    def __init__(self, chips):
+        me = lax.axis_index("dp")
+        self.chips = chips
+        self.core = me % 2
+        chip = me // 2
+        column = chip % 2
+        self.place = (1 - column) * (chip // 2) + column * (chips - 1 - chip // 2)
+        self.turn = 1 - 2 * self.core
+        self.ahead = 2 * chip_of(self.place + self.turn, chips) + self.core
+        self.behind = 2 * chip_of(self.place - self.turn, chips) + self.core
+        self.across = 2 * chip + 1 - self.core
+
+    def barrier(self):
+        semaphore = pltpu.get_barrier_semaphore()
+        for device in (self.ahead, self.behind, self.across):
+            pl.semaphore_signal(
+                semaphore, inc=1, device_id={"dp": device}, device_id_type=pl.DeviceIdType.MESH
+            )
+        pl.semaphore_wait(semaphore, 3)
+
+    def chip_at(self, steps):
+        return chip_of(self.place + self.turn * steps, self.chips)
+
+
+def cuts_of(share):
+    return max(c for c in range(1, 5) if share % (8 * c) == 0)
+
+
+class Reduce:
+    def __init__(self, make, own, keep, sent, other, slot, swap_send, swap_recv, ring_send, ring_recv):
+        self.make = make
+        self.keep, self.sent, self.own, self.other, self.slot = keep, sent, own, other, slot
+        self.swap_sems, self.ring_sems = (swap_send, swap_recv), (ring_send, ring_recv)
+        self.chips, share = slot.shape[0], slot.shape[1]
+        self.cuts = ring_send.shape[0]
+        self.piece = share // self.cuts
+        self.at = Place(self.chips)
+
+    @staticmethod
+    def scratch(chips, share, width):
+        dma = pltpu.SemaphoreType.DMA
+        cuts = cuts_of(share)
+        return [pltpu.VMEM((chips, share, width), f32)] * 4 + (
+            [dma((chips,))] * 2 + [dma((cuts, chips - 1))] * 2
+        )
+
+    def part(self, cut):
+        return pl.ds(pl.multiple_of(cut * self.piece, 8), self.piece)
+
+    def swap(self, step, sign):
+        tile = self.at.chip_at(sign * (step + 1))
+        send, receive = self.swap_sems
+        return remote(
+            self.sent.at[tile], self.other.at[tile], send.at[step], receive.at[step], self.at.across
+        )
+
+    def ring(self, cut, step):
+        send, receive = self.ring_sems
+        part = self.part(cut)
+        return remote(
+            self.slot.at[step, part],
+            self.slot.at[step + 1, part],
+            send.at[cut, step],
+            receive.at[cut, step],
+            self.at.ahead,
+        )
+
+    def prepare(self, step):
+        @pl.when(2 * (step + 1) < self.chips)
+        def _():
+            self.make(self.at.chip_at(step + 1))
+            self.swap(step, 1).start()
+            self.make(self.at.chip_at(-(step + 1)))
+
+        @pl.when(2 * (step + 1) == self.chips)
+        def _():
+            self.make(self.at.chip_at(step + 1))
+            self.swap(step, 1).start()
+
+        @pl.when((2 * (step + 1) > self.chips) & (step < self.chips - 1))
+        def _():
+            self.swap(step, 1).start()
+
+        @pl.when(step == self.chips - 1)
+        def _():
+            self.make(self.at.chip_at(0))
+            self.swap(step, 1).start()
+
+    def unit(self, step, cut):
+        part = self.part(cut)
+        tile = self.at.chip_at(-(step + 1))
+
+        @pl.when(step == 0)
+        def _():
+            self.slot[0, part] = self.keep[tile, part] + self.other[tile, part]
+
+        @pl.when(step > 0)
+        def _():
+            self.ring(cut, step - 1).wait_recv()
+            self.slot[step, part] += self.keep[tile, part] + self.other[tile, part]
+
+        @pl.when(step < self.chips - 1)
+        def _():
+            self.ring(cut, step).start()
+
+        @pl.when(step == self.chips - 1)
+        def _():
+            self.own[part] = self.slot[step, part]
+
+    def run(self):
+        self.at.barrier()
+        self.prepare(0)
+
+        def body(step, carry):
+            @pl.when(step < self.chips - 1)
             def _():
-                ring_copy(w, c, s).start()
-            @pl.when(s == chips - 1)
+                self.prepare(step + 1)
+
+            self.swap(step, -1).wait_recv()
+            for cut in range(self.cuts):
+                self.unit(step, cut)
+            return carry
+
+        lax.fori_loop(0, self.chips, body, 0)
+
+        def sent(step, carry):
+            self.swap(step, 1).wait_send()
+
+            @pl.when(step < self.chips - 1)
             def _():
-                own = slot[w].at[chips - 1, part(w, c)]
-                remote(own, out_at(w, c, 0), pass_send.at[w, c, 0], pass_recv.at[w, c, 0], ahead).start()
-                remote(own, out_at(w, c, 0), give_send.at[w, c, 0], give_recv.at[w, c, 0], across).start()
-                pltpu.make_async_copy(own, out_at(w, c, 0), store.at[w, c]).start()
-        return carry
-    lax.fori_loop(1, chips, reduce_step, 0)
-    def pass_copy(w, c, s):
-        return remote(out_at(w, c, s), out_at(w, c, s), pass_send.at[w, c, s], pass_recv.at[w, c, s], ahead)
-    def give_copy(w, c, s):
-        return remote(out_at(w, c, s), out_at(w, c, s), give_send.at[w, c, s], give_recv.at[w, c, s], across)
-    def gather_step(s, carry):
-        for w, c in pieces:
-            at = out_at(w, c, s)
-            remote(at, at, pass_send.at[w, c, s - 1], pass_recv.at[w, c, s - 1], ahead).wait_recv()
-            @pl.when(s < chips - 1)
+                for cut in range(self.cuts):
+                    self.ring(cut, step).wait_send()
+
+            return carry
+
+        lax.fori_loop(0, self.chips, sent, 0)
+
+
+class Gather:
+    def __init__(self, own, out, pass_send, pass_recv, give_send, give_recv, store):
+        self.own, self.out, self.store = own, out, store
+        self.pass_sems, self.give_sems = (pass_send, pass_recv), (give_send, give_recv)
+        self.chips = out.shape[0]
+        self.cuts = store.shape[0]
+        self.piece = own.shape[0] // self.cuts
+        self.units = (self.chips - 1) * self.cuts
+        self.at = Place(self.chips)
+
+    @staticmethod
+    def specs(own, chips):
+        share, width = own.shape
+        cuts = cuts_of(share)
+        dma = pltpu.SemaphoreType.DMA
+        return (
+            [pl.BlockSpec(memory_space=pltpu.VMEM)],
+            [pl.BlockSpec(memory_space=pl.ANY)],
+            [jax.ShapeDtypeStruct((chips, 2, share, width), f32)],
+            [dma((cuts, chips - 1))] * 2 + [dma((cuts, chips))] * 2 + [dma((cuts,))],
+        )
+
+    def part(self, cut):
+        return pl.ds(pl.multiple_of(cut * self.piece, 8), self.piece)
+
+    def tile(self, cut, behind):
+        return self.out.at[self.at.chip_at(-behind), self.at.core, self.part(cut)]
+
+    def onward(self, source, cut, behind):
+        send, receive = self.pass_sems
+        return remote(
+            source, self.tile(cut, behind), send.at[cut, behind], receive.at[cut, behind], self.at.ahead
+        )
+
+    def give(self, source, cut, behind):
+        send, receive = self.give_sems
+        return remote(
+            source, self.tile(cut, behind), send.at[cut, behind], receive.at[cut, behind], self.at.across
+        )
+
+    def keep(self, cut):
+        return pltpu.make_async_copy(
+            self.own.at[self.part(cut)], self.tile(cut, 0), self.store.at[cut]
+        )
+
+    def start(self):
+        self.at.barrier()
+
+        def body(cut, carry):
+            source = self.own.at[self.part(cut)]
+            self.onward(source, cut, 0).start()
+            self.give(source, cut, 0).start()
+            self.keep(cut).start()
+            return carry
+
+        lax.fori_loop(0, self.cuts, body, 0)
+
+    def unit(self, index):
+        behind, cut = 1 + index // self.cuts, index % self.cuts
+        here = self.tile(cut, behind)
+        send, receive = self.pass_sems
+        remote(
+            here, here, send.at[cut, behind - 1], receive.at[cut, behind - 1], self.at.ahead
+        ).wait_recv()
+
+        @pl.when(behind < self.chips - 1)
+        def _():
+            self.onward(here, cut, behind).start()
+
+        self.give(here, cut, behind).start()
+
+    def run(self, first, last):
+        def body(index, carry):
+            self.unit(index)
+            return carry
+
+        lax.fori_loop(first, last, body, 0)
+
+    def finish(self):
+        send, receive = self.give_sems
+
+        def body(index, carry):
+            cut, behind = index // self.chips, index % self.chips
+            here = self.tile(cut, behind)
+
+            @pl.when(behind < self.chips - 1)
             def _():
-                pass_copy(w, c, s).start()
-            give_copy(w, c, s).start()
-        return carry
-    lax.fori_loop(1, chips, gather_step, 0)
-    def drain(s, carry):
-        for w in range(count):
-            swap_copy(w, s).wait_send()
-        for w, c in pieces:
-            @pl.when(s < chips - 1)
+                self.onward(here, cut, behind).wait_send()
+
+            self.give(here, cut, behind).wait_send()
+            theirs = self.out.at[self.at.chip_at(behind), 1 - self.at.core, self.part(cut)]
+            remote(
+                theirs, theirs, send.at[cut, behind], receive.at[cut, behind], self.at.across
+            ).wait_recv()
+
+            @pl.when(behind == 0)
             def _():
-                ring_copy(w, c, s).wait_send()
-                pass_copy(w, c, s).wait_send()
-            give_copy(w, c, s).wait_send()
-            theirs = out[w].at[chip_of(place + turn * s, chips), 1 - core, part(w, c)]
-            remote(theirs, theirs, give_send.at[w, c, s], give_recv.at[w, c, s], across).wait_recv()
-        return carry
-    lax.fori_loop(0, chips, drain, 0)
-    for w, c in pieces:
-        pltpu.make_async_copy(slot[w].at[chips - 1, part(w, c)], out_at(w, c, 0), store.at[w, c]).wait()
-
-def ring_sum(tiles, collective_id, cut=4):
-    count = len(tiles)
-    chips = tiles[0][0].shape[0]
-    cuts = []
-    for keep, _ in tiles:
-        share = keep.shape[1]
-        cuts.append(max(c for c in range(1, cut + 1) if share % (8 * c) == 0))
-    hbm = pl.BlockSpec(memory_space=pl.ANY); vmem = pl.BlockSpec(memory_space=pltpu.VMEM)
-    dma = lambda *s: pltpu.SemaphoreType.DMA(s)
-    most = max(cuts)
-    outs = pl.pallas_call(
-        functools.partial(ring_kernel, chips, count, tuple(cuts)),
-        in_specs=[vmem] * count + [hbm] * count,
-        out_specs=[hbm] * count,
-        out_shape=[jax.ShapeDtypeStruct((chips, 2) + k.shape[1:], f32) for k, _ in tiles],
-        scratch_shapes=[pltpu.VMEM(k.shape, f32) for k, _ in tiles] * 2
-        + [dma(count, chips)] * 2 + [dma(count, most, chips)] * 6 + [dma(count, most)],
+                self.keep(cut).wait()
+
+            return carry
+
+        lax.fori_loop(0, self.cuts * self.chips, body, 0)
+
+
+def riding(kernel, inputs, outputs, scratch, steps, marks):
+    def body(*refs):
+        ins, own, rest = refs[:inputs], refs[inputs], refs[inputs + 1 :]
+        outs, full, rest = rest[:outputs], rest[outputs], rest[outputs + 1 :]
+        own_scratch, extra = rest[:scratch], rest[scratch:]
+        rider = Gather(own, full, *extra)
+        step = pl.program_id(0)
+        total = steps * marks
+
+        @pl.when(step == 0)
+        def _():
+            rider.start()
+
+        def mark(number):
+            at = step * marks + number
+            rider.run(at * rider.units // total, (at + 1) * rider.units // total)
+
+        kernel(*ins, *outs, *own_scratch, mark=mark)
+
+        @pl.when(step == steps - 1)
+        def _():
+            rider.finish()
+
+    return body
+
+
+def gather_kernel_alone(own, out, *sems):
+    rider = Gather(own, out, *sems)
+    rider.start()
+    rider.run(0, rider.units)
+    rider.finish()
+
+
+def gather_alone(own, chips, collective_id):
+    ins, outs, shapes, scratch = Gather.specs(own, chips)
+    return pl.pallas_call(
+        gather_kernel_alone,
+        in_specs=ins,
+        out_specs=outs,
+        out_shape=shapes,
+        scratch_shapes=scratch,
         compiler_params=pltpu.CompilerParams(collective_id=collective_id, has_side_effects=True),
-        name="ring_sum",
-    )(*[k for k, _ in tiles], *[s for _, s in tiles])
-    return [o.reshape(-1, o.shape[-1]) for o in outs]
+        cost_estimate=cost(40_000_000_000, 10_000_000),
+        name="gather",
+    )(own)[0]
+
+
+def product(lefts, rights, block, chip, per):
+    at = pl.ds(pl.multiple_of(chip // per * block, LANES), block)
+    total = tn_dot(lefts[0][:, at], rights[0][...])
+    for left, right in zip(lefts[1:], rights[1:]):
+        total = total + tn_dot(left[:, at], right[...])
+    return total
+
+
+def block_of(height, chips):
+    block = max(LANES, height // chips)
+    return block, block * chips // height
+
+
+def weight_kernel(images, *refs):
+    lefts, rights = refs[:images], refs[images : 2 * images]
+    own, keep, sent, other, slot, work, *sems = refs[2 * images :]
+    chips, share = slot.shape[0], slot.shape[1]
+    block, per = block_of(lefts[0].shape[1], chips)
+    core = lax.axis_index("dp") % 2
+
+    def make(chip):
+        work[...] = product(lefts, rights, block, chip, per)
+        first = chip % per * 2
+        keep[chip] = work[pl.ds(pl.multiple_of((first + core) * share, 8), share), :]
+        sent[chip] = work[pl.ds(pl.multiple_of((first + 1 - core) * share, 8), share), :]
+
+    Reduce(make, own, keep, sent, other, slot, *sems).run()
+
+
+def reducing(kernel, operands, chips, share, width, work, collective_id):
+    arrays = Reduce.scratch(chips, share, width)
+    whole = pl.BlockSpec(memory_space=pltpu.VMEM)
+    return pl.pallas_call(
+        kernel,
+        in_specs=[whole] * len(operands),
+        out_specs=whole,
+        out_shape=jax.ShapeDtypeStruct((share, width), f32),
+        scratch_shapes=arrays[:4] + work + arrays[4:],
+        compiler_params=pltpu.CompilerParams(collective_id=collective_id, has_side_effects=True),
+        cost_estimate=cost(40_000_000_000, 20_000_000),
+    )(*operands)
+
+
+def weight_grad(lefts, rights, chips, collective_id):
+    height, width = lefts[0].shape[1], rights[0].shape[1]
+    block, _ = block_of(height, chips)
+    return reducing(
+        functools.partial(weight_kernel, len(lefts)), [*lefts, *rights], chips,
+        height // (2 * chips), width, [pltpu.VMEM((block, width), f32)], collective_id,
+    )
+
+
+def heads_kernel(images, *refs):
+    layers, stacks, attended, lows = (refs[k * images : (k + 1) * images] for k in range(4))
+    small, own, keep, sent, other, slot, work, work_two, *sems = refs[4 * images :]
+    chips, part = slot.shape[0], slot.shape[2]
+    core = lax.axis_index("dp") % 2
+    block, per = block_of(layers[0].shape[1], chips)
+    block_two, per_two = block_of(attended[0].shape[1], chips)
+    share, mixing = block // (2 * per), block_two // (2 * per_two)
+
+    def split(source, chip, per, share, columns, rows, lanes):
+        first = chip % per * 2
+        for target, which in ((keep, core), (sent, 1 - core)):
+            target[chip, rows, lanes] = source[
+                pl.ds(pl.multiple_of((first + which) * share, 8), share), columns
+            ]
+
+    def make(chip):
+        work[...] = product(layers, stacks, block, chip, per)
+        for which in range(3):
+            for pair in range(part // PAIR):
+                split(
+                    work, chip, per, share, pl.ds((3 * pair + which) * PAIR, PAIR),
+                    pl.ds(which * share, share), pl.ds(pair * PAIR, PAIR),
+                )
+        work_two[...] = product(attended, lows, block_two, chip, per_two)
+        at = 3 * share
+        for piece in range(work_two.shape[1] // part):
+            split(
+                work_two, chip, per_two, mixing, pl.ds(piece * part, part), pl.ds(at, mixing),
+                pl.ds(0, part),
+            )
+            at += mixing
+        rest = pl.ds(at, keep.shape[1] - at)
+        keep[chip, rest, :] = small[chip, core]
+        sent[chip, rest, :] = small[chip, 1 - core]
+
+    Reduce(make, own, keep, sent, other, slot, *sems).run()
+
+
+def heads_grad(layers, stacks, attended, lows, small, chips, collective_id):
+    height, wide = layers[0].shape[1], stacks[0].shape[1]
+    part = wide // 3
+    mixing_height, mixing_width = attended[0].shape[1], lows[0].shape[1]
+    share = (height * 3 + mixing_height * mixing_width // part) // (2 * chips) + small.shape[2]
+    work = [
+        pltpu.VMEM((block_of(height, chips)[0], wide), f32),
+        pltpu.VMEM((block_of(mixing_height, chips)[0], mixing_width), f32),
+    ]
+    return reducing(
+        functools.partial(heads_kernel, len(layers)),
+        [*layers, *stacks, *attended, *lows, small], chips, share, part, work, collective_id,
+    )
 
 
 def output_kernel(hidden_ref, own_ref, other_ref, bias_ref, *out):
@@ -577,8 +851,8 @@
     ).astype(bf16)
 
 
-def finish(kernel, name, image, shape, operands, before):
-    images, length, width = shape
+def finish(kernel, image, shape, operands, before):
+    _, length, width = shape
     picture = pl.BlockSpec((None, length, width), lambda j: (image, 0, 0))
 
     def spec(array):
@@ -593,7 +867,6 @@
         out_shape=jax.ShapeDtypeStruct(shape, bf16),
         input_output_aliases={len(operands): 0} if extra else {},
         cost_estimate=cost(10_000_000, 10_000_000),
-        name=name,
     )(*operands, *extra)
 
 
@@ -601,7 +874,7 @@
     return lax.ppermute(array, "tensor", [(0, 1), (1, 0)])
 
 
-def on_device(
+def layer(
     block_input,
     first_scale,
     first_shift,
@@ -628,7 +901,6 @@
     core = lax.axis_index("dp") % 2
     cores = [(i, i ^ 1) for i in range(size)]
     place = jnp.stack([owner, core]).astype(jnp.int32)
-    which = core.astype(jnp.int32).reshape(1)
     first_scale, first_shift, mixing_bias, second_scale, second_shift, shrink_bias = (
         v.reshape(1, width)
         for v in (first_scale, first_shift, mixing_bias, second_scale, second_shift, shrink_bias)
@@ -650,37 +922,40 @@
     each_image = range(images)
     layer_one, qkv, attended, wide, logsum = zip(
         *[
-            attend(i, rows, block_input, joined, joined_bias, first_scale, first_shift)
+            attend(
+                i, rows, block_input, joined, joined_bias, first_scale,
+                first_shift,
+            )
             for i in each_image
         ]
     )
     hidden_one, layer_two, upstream, activated, pre_low, expand_sums, shrunk, partial_two = zip(
         *[
             feed(
-                i, place, block_input, attended[i], swap(wide[i]), full_mixing, mixing_bias,
+                i, place, block_input, attended[i],
+                swap(wide[i]), full_mixing, mixing_bias,
                 second_scale, second_shift, output_grad, expand_weight,
                 expand_bias.reshape(1, hidden), shrink_weight,
             )
             for i in each_image
         ]
     )
-    shrink_tiles = weight_grad(activated, upstream, which, chips)
-    expand_tiles = weight_grad(layer_two, pre_low, which, chips)
-    (shrink_full,) = ring_sum([shrink_tiles], 1)
-
+    shrunk_other = [swap(shrunk[i]) for i in each_image]
+    backs, sums = [], []
+    for i, (left, right) in enumerate(((activated, upstream), (layer_two, pre_low))):
+        own_tile = weight_grad(left, right, chips, 4 * i + 1)
+        *back, full = attend_back(
+            i, partial_two[i], swap(partial_two[i]),
+            hidden_one[i], upstream[i], mixing_weight, qkv[i], logsum[i], joined, block_input,
+            second_scale, own_tile, chips, 4 * i + 2,
+        )
+        backs.append(back)
+        sums.append(full)
+    shrink_full, expand_full = (s.reshape(-1, s.shape[-1]) for s in sums)
     (
         hidden_grad, hidden_low, stacked, query_bias, value_bias, partial_one, sums_two, sums_one,
-    ) = zip(
-        *[
-            attend_back(
-                i, partial_two[i], swap(partial_two[i]), hidden_one[i], upstream[i], mixing_weight,
-                qkv[i], logsum[i], joined, block_input, second_scale,
-            )
-            for i in each_image
-        ]
-    )
-    heads_tiles = weight_grad(layer_one, stacked, which, chips)
-    mixing_tiles = weight_grad(attended, hidden_low, which, chips)
+    ) = zip(*backs)
+    partial_other = [swap(partial_one[i]) for i in each_image]
     small = jnp.concatenate(
         [
             sum(query_bias).reshape(-1),
@@ -691,33 +966,35 @@
         ]
     )
     each = -(-small.shape[0] // size)
-    chunk = -(-each // (8 * LANES)) * 8 * LANES
+    chunk = -(-each // (8 * local)) * 8 * local
     small_tiles = jnp.pad(small, (0, each * size - small.shape[0])).reshape(size, each)
     small_tiles = jnp.pad(small_tiles, ((0, 0), (0, chunk - each))).reshape(
-        chips, 2, chunk // LANES, LANES
-    )
-    small_pair = (
-        lax.dynamic_index_in_dim(small_tiles, core, 1, keepdims=False),
-        lax.dynamic_index_in_dim(small_tiles, 1 - core, 1, keepdims=False),
-    )
-    heads_full, expand_full, mixing_full, small_full = ring_sum(
-        [heads_tiles, expand_tiles, mixing_tiles, small_pair], 2
-    )
+        chips, 2, chunk // local, local
+    )
+    heads_own = heads_grad(layer_one, stacked, attended, hidden_low, small_tiles, chips, 9)
+    heads_all = gather_alone(heads_own, chips, 10).reshape(size, -1, local)
+    share = width // size
     heads_full = (
-        heads_full.reshape(width, pairs, 3, PAIR).transpose(0, 2, 1, 3).reshape(width, 3, local)
-    )
-    small = small_full.reshape(size, chunk)[:, :each].reshape(-1)
+        heads_all[:, : 3 * share].reshape(size, 3, share, local).transpose(0, 2, 1, 3)
+    ).reshape(width, 3, local)
+    end = 3 * share + local * width // (size * local)
+    mixing_full = (
+        heads_all[:, 3 * share : end]
+        .reshape(size, width // local, local // size, local)
+        .transpose(0, 2, 1, 3)
+    ).reshape(local, width)
+    small = heads_all[:, end:].reshape(size, chunk)[:, :each].reshape(-1)
 
     block_output = input_grad = None
     for i in each_image:
         block_output = finish(
-            output_kernel, "output", i, block_input.shape,
-            [hidden_one[i], shrunk[i], swap(shrunk[i]), shrink_bias], block_output,
+            output_kernel, i, block_input.shape,
+            [hidden_one[i], shrunk[i], shrunk_other[i], shrink_bias], block_output,
         )
     for i in each_image:
         input_grad = finish(
-            input_kernel, "input", i, block_input.shape,
-            [hidden_grad[i], partial_one[i], swap(partial_one[i]), block_input, first_scale],
+            input_kernel, i, block_input.shape,
+            [hidden_grad[i], partial_one[i], partial_other[i], block_input, first_scale],
             input_grad,
         )
 
@@ -763,7 +1040,7 @@
         P("dp", None, None),
     )
     return jax.shard_map(
-        on_device,
+        layer,
         mesh=mesh,
         in_specs=placed,
         out_specs=(

time: 612 us -> 599 us (0.979)
  Pallas kernels: 471 us -> 431 us
  waiting for transfers between devices: 43.7 us -> 76.5 us
  local copies, waits for them, and re-layouts: 71.6 us -> 64.3 us
    pallas_call x8 -> x6, Pallas kernels: 364 us -> 324 us  [the longest x3 162 us: reducing(): pl.pallas_call(kernel, in_specs=[whole] * len(operands), out_specs=whole,...]
    ppermute x10, waiting for transfers between devices: 43.7 us -> 76.5 us  [swap(): return lax.ppermute(array, 'tensor', [(0, 1), (1, 0)])]
    another operation x3 -> x2, local copies, waits for them, and re-layouts: 11.4 us -> 0.84 us  [layer(): jnp.stack([heads_bias[0].reshape(pairs, PAIR), zero_bias, heads_bias[1].r...]
    slice x6 -> x9, local copies, waits for them, and re-layouts: 2.5 us -> 11.8 us  [the longest x1 6.47 us: layer(): heads_all[:, :3 * share].reshape(size, 3, share, local)]
    transpose x2 -> x1, local copies, waits for them, and re-layouts: 11.5 us -> 2.45 us  [layer(): heads_weight.reshape(width, 3, pairs, PAIR).transpose(0, 2, 1, 3)]
    reshape x4 -> x6, local copies, waits for them, and re-layouts: 3.7 us -> 12.1 us  [the longest x1 6.74 us: layer(): heads_all[:, :3 * share].reshape(size, 3, share, local)]
    unnamed x42 -> x40, local copies, waits for them, and re-layouts: 42 us -> 37.1 us
  transfers between devices with their start and end apart: 11 -> 11, of which waited for: 4 -> 3; matrix products, arithmetic and copies ran while one was open for 9% -> 8% of each run, Pallas kernels for 77% -> 72%
where the time goes in v2:
time: 599 us; the launch traced here: 592 us
  Pallas kernels  431 us (72%)
  waiting for transfers between devices  76.5 us (13%)
  local copies, waits for them, and re-layouts  64.3 us (11%)
  starting transfers between devices  11.9 us (2%)
  other arithmetic  6.84 us (1%)
    pallas_call x3, Pallas kernels, reducing(): pl.pallas_call(kernel, in_specs=[whole] * len(operands), out_specs=whole,...  162 us
    pallas_call x2, Pallas kernels, attend_back(): pl.pallas_call(riding(kernel, len(in_specs), len(out_specs), len(scratch)...  115 us
    ppermute x10, waiting for transfers between devices, swap(): return lax.ppermute(array, 'tensor', [(0, 1), (1, 0)])  76.5 us
    pallas_call x1, Pallas kernels, gather_alone(): pl.pallas_call(gather_kernel_alone, in_specs=ins, out_specs=outs, out_sha...  47.7 us
    pallas_call x2, Pallas kernels, feed(): pl.pallas_call(feed_kernel, grid=(hidden // tile,), in_specs=[pl.BlockSpe...  46.4 us
    unnamed x40, local copies, waits for them, and re-layouts  37.1 us
    pallas_call x2, Pallas kernels, attend(): pl.pallas_call(functools.partial(attend_kernel, length, chunks), grid=(pa...  36 us
    pallas_call x4, Pallas kernels, finish(): pl.pallas_call(kernel, grid=(1,), in_specs=[spec(a) for a in operands] +...  21.1 us
  transfers between devices with their start and end apart: 11, of which 3 were waited for; matrix products, arithmetic and copies ran while one was open for 8% of the time, Pallas kernels for 72%

profile of v2, /device:TPU:0, one launch (start us, length us, event | category | flops | bytes accessed | tf_op | source)
XLA Modules:
  0.0 591.6 jit_solution(12023888571965254759)
XLA Ops:
  0.7 2.1 dynamic-slice_convert_fusion
  2.8 3.0 collective-permute-start.1
  5.8 0.8 slice_bitcast_fusion.1
  7.3 3.9 copy.73.input_ref.refs_8_
  11.2 3.0 copy.67
  14.2 2.4 copy.68
  16.6 2.9 copy.72.weight_ref.refs_7_
  19.6 17.9 %attend.2 = (bf16[592,1024]{1,0:T(8,128)(2,1)}, bf16[592,1536]{1,0:T(8,128)(2,1)}, bf16[592,512]{1,0:T(8,128)(2,1)}, f32[592,512]{1,0:T(8,128)}, f32[4,5,1,256]{3,2,1,0:T(1,128)}) custom-call(bf16[2,577,1024]{2,1,0:T(8,128)(2,1)} %copy.73.input_ref.refs_8_, bf16[1024,1536]{1,0:T(8,128)(2,1)} %copy.72.weight_ref.refs_7_, f32[1,1536]{1,0:T(1,128)} %reshape.112.bias_ref, ...), custom_call_target="tpu_custom_call" | custom-call | flops 10000000000 | bytes 10000000 | tf_op jit(solution)/shard_map/attend/pallas_call | solution.py:125
  37.6 18.1 %attend.3 = (bf16[592,1024]{1,0:T(8,128)(2,1)}, bf16[592,1536]{1,0:T(8,128)(2,1)}, bf16[592,512]{1,0:T(8,128)(2,1)}, f32[592,512]{1,0:T(8,128)}, f32[4,5,1,256]{3,2,1,0:T(1,128)}) custom-call(bf16[2,577,1024]{2,1,0:T(8,128)(2,1)} %copy.73.input_ref.refs_8_, bf16[1024,1536]{1,0:T(8,128)(2,1)} %copy.72.weight_ref.refs_7_, f32[1,1536]{1,0:T(1,128)} %reshape.112.bias_ref, ...), custom_call_target="tpu_custom_call" | custom-call | flops 10000000000 | bytes 10000000 | tf_op jit(solution)/shard_map/attend/pallas_call | solution.py:125
  55.8 1.8 collective-permute-start.4
  57.6 2.2 copy.74.upstream_ref
  60.4 1.0 copy-done.2
  61.3 3.4 gather_weight.1.mixing_ref
  64.7 2.7 collective-permute-done.other_ref
  67.4 23.1 %feed.2 = (f32[592,1024]{1,0:T(8,128)}, bf16[592,1024]{1,0:T(8,128)(2,1)}, bf16[592,1024]{1,0:T(8,128)(2,1)}, bf16[592,2048]{1,0:T(8,128)(2,1)}, bf16[592,2048]{...) custom-call(s32[2]{0:T(128)} %pad_add_fusion.place_ref, ...), custom_call_target="tpu_custom_call" | custom-call | flops 11000000512 | bytes 25000000 | tf_op jit(solution)/shard_map/feed/pallas_call | solution.py:389
  90.7 1.9 collective-permute-start.6
  92.9 23.3 %feed.3 = (f32[592,1024]{1,0:T(8,128)}, bf16[592,1024]{1,0:T(8,128)(2,1)}, bf16[592,1024]{1,0:T(8,128)(2,1)}, bf16[592,2048]{1,0:T(8,128)(2,1)}, bf16[592,2048]{...) custom-call(s32[2]{0:T(128)} %pad_add_fusion.place_ref, ...), custom_call_target="tpu_custom_call" | custom-call | flops 11000000512 | bytes 25000000 | tf_op jit(solution)/shard_map/feed/pallas_call | solution.py:389
  116.6 1.7 collective-permute-start.8
  118.3 1.3 add.31
  119.6 53.2 %shard_map.248.refs_10_ = f32[128,1024]{1,0:T(8,128)} custom-call(bf16[592,2048]{1,0:T(8,128)(2,1)} %get-tuple-element.80.refs_0_, bf16[592,2048]{1,0:T(8,128)(2,1)} %get-tuple-element.81.refs_1_, bf16[592,1024]{1,0:T(8,128)(2,1)} %get-tuple-element.77.refs_2_.refs_3_, bf16[592,1024]{1,0:T(8,128)(2,1)} %get-tuple-element.67.refs_3_), custom_call_target="tpu_custom_call" | custom-call | flops 40000000000 | bytes 20000000 | tf_op jit(solution)/shard_map/pallas_call | solution.py:762
  172.9 53.4 %shard_map.247.refs_10_ = f32[64,2048]{1,0:T(8,128)} custom-call(bf16[592,1024]{1,0:T(8,128)(2,1)} %get-tuple-element.70.refs_0_, bf16[592,1024]{1,0:T(8,128)(2,1)} %get-tuple-element.71.refs_1_, bf16[592,2048]{1,0:T(8,128)(2,1)} %get-tuple-element.72.refs_2_, bf16[592,2048]{1,0:T(8,128)(2,1)} %get-tuple-element.73.refs_3_), custom_call_target="tpu_custom_call" | custom-call | flops 40000000000 | bytes 20000000 | tf_op jit(solution)/shard_map/pallas_call | solution.py:762
  226.3 73.5 %collective-permute-done.8.refs_1_ = f32[592,1024]{1,0:T(8,128)} collective-permute-done((f32[592,1024]{1,0:T(8,128)}, f32[592,1024]{1,0:T(8,128)}, u32[]{:S(2)}, u32[]{:S(2)}) %collective-permute-start.8) | collective-permute-done | bytes 2424864 | tf_op jit(solution)/shard_map/ppermute | solution.py:874
  299.8 57.1 %attend_back.3 = (f32[592,1024]{1,0:T(8,128)}, bf16[592,1024]{1,0:T(8,128)(2,1)}, bf16[592,1536]{1,0:T(8,128)(2,1)}, f32[1,512]{1,0:T(1,128)}, f32[1,512]{1,0:T(...) custom-call(f32[592,1024]{1,0:T(8,128)} %get-tuple-element.76.refs_0_, ...), custom_call_target="tpu_custom_call" | custom-call | flops 40000000000 | bytes 20000000 | tf_op jit(solution)/shard_map/attend_back/pallas_call | solution.py:284
  357.0 1.4 copy-done.10
  358.4 57.5 %attend_back.2 = (f32[592,1024]{1,0:T(8,128)}, bf16[592,1024]{1,0:T(8,128)(2,1)}, bf16[592,1536]{1,0:T(8,128)(2,1)}, f32[1,512]{1,0:T(1,128)}, f32[1,512]{1,0:T(...) custom-call(f32[592,1024]{1,0:T(8,128)} %get-tuple-element.66.refs_0_, ...), custom_call_target="tpu_custom_call" | custom-call | flops 40000000000 | bytes 20000000 | tf_op jit(solution)/shard_map/attend_back/pallas_call | solution.py:284
  415.9 0.7 add_bitcast_fusion.1
  416.6 0.7 add_bitcast_fusion
  417.4 0.7 add.30
  418.0 0.6 add.29
  418.8 0.9 copy.91
  420.3 1.4 collective-permute-start.9
  421.7 55.1 %shard_map.251.own = f32[264,512]{1,0:T(8,128)} custom-call(bf16[592,1024]{1,0:T(8,128)(2,1)} %get-tuple-element.84.refs_0_, bf16[592,1024]{1,0:T(8,128)(2,1)} %get-tuple-element.85.refs_1_, bf16[592,1536]{1,0:T(8,128)(2,1)} %get-tuple-element.86.refs_2_, bf16[592,1536]{1,0:T(8,128)(2,1)} %get-tuple-element.87.refs_3_, ...), custom_call_target="tpu_custom_call" | custom-call | flops 40000000000 | bytes 20000000 | tf_op jit(solution)/shard_map/pallas_call | solution.py:762
  476.8 47.7 %gather.1 = f32[8,2,264,512]{3,2,1,0:T(8,128)} custom-call(f32[264,512]{1,0:T(8,128)} %shard_map.251.own), custom_call_target="tpu_custom_call" | custom-call | flops 40000000000 | bytes 10000000 | tf_op jit(solution)/shard_map/gather/pallas_call | solution.py:718
  524.5 1.0 slice.69
  526.4 0.7 collective-permute-start.10
  527.7 1.9 slice.72
  529.6 6.5 %slice.68 = f32[16,192,512]{2,1,0:T(8,128)} slice(f32[16,264,512]{2,1,0:T(8,128)} %bitcast.59), slice={[0:16], [0:192], [0:512]} | slice | bytes 12582912 | tf_op jit(solution)/shard_map/slice | solution.py:978
  536.1 4.5 shard_map.245.out_0_
  540.6 4.5 shard_map.246
  545.1 5.5 copy.87
  551.2 6.7 %copy.85 = f32[16,3,64,512]{3,2,0,1:T(8,128)} copy(f32[16,3,64,512]{3,2,1,0:T(8,128)} %bitcast.54) | data formatting | bytes 12582912 | tf_op jit(solution)/shard_map/reshape | solution.py:978
  557.9 1.6 copy.86
  559.5 1.8 copy.93
  561.9 6.1 %shard_map.249.out_0_ = bf16[2,577,1024]{2,1,0:T(8,128)(2,1)} custom-call(f32[592,1024]{1,0:T(8,128)} %get-tuple-element.82.grad_ref, f32[592,1024]{1,0:T(8,128)} %get-tuple-element.83.own_ref, f32[592,1024]{1,0:T(8,128)} %collective-permute-done.9.other_ref, bf16[2,577,1024]{2,1,0:T(8,128)(2,1)} %copy.73.input_ref.refs_8_, f32[1,1024]{1,0:T(1,128)} %bitcast.81), custom_call_target="tpu_custom_call" | custom-call | flops 10000000 | bytes 10000000 | tf_op jit(solution)/shard_map/pallas_call | solution.py:862
  568.0 6.1 %shard_map.250 = bf16[2,577,1024]{2,1,0:T(8,128)(2,1)} custom-call(f32[592,1024]{1,0:T(8,128)} %get-tuple-element.74.grad_ref, f32[592,1024]{1,0:T(8,128)} %get-tuple-element.75.own_ref, f32[592,1024]{1,0:T(8,128)} %collective-permute-done.7.other_ref, bf16[2,577,1024]{2,1,0:T(8,128)(2,1)} %copy.73.input_ref.refs_8_, ...), custom_call_target="tpu_custom_call", output_to_operand_aliasing={{}: (5, {})} | custom-call | flops 10000000 | bytes 10000000 | tf_op jit(solution)/shard_map/pallas_call | solution.py:862
  574.1 5.9 copy.88
  580.0 8.0 %copy.105 = f32[1024,2048]{1,0:T(8,128)} copy(f32[1024,2048]{1,0:T(8,128)} %bitcast.63) | data formatting | bytes 16777216
  588.0 3.4 copy.106
  (61 shorter events, 5.9 us)
Async XLA Ops:
  2.8 8.4 %copy-start = (bf16[1024,3,512]{2,0,1:T(8,128)(2,1)S(1)}, bf16[1024,3,512]{2,0,1:T(8,128)(2,1)}, u32[]{:S(2)}) copy-start(bf16[1024,3,512]{2,0,1:T(8,128)(2,1)} %param.17) | copy-start | bytes 9437188
  2.8 34.8 %collective-permute-start.1 = (f32[256,1024]{1,0:T(8,128)}, f32[256,1024]{1,0:T(8,128)}, u32[]{:S(2)}, u32[]{:S(2)}) collective-permute-start(f32[256,1024]{1,0:T(8,128)} %dynamic-slice_convert_fusion), channel_id=1, source_target_pairs={{0,1},{1,0},{2,3},{3,2},{4,5},{5,4},{6,7},{7,6},{8,9},{9,8},{10,11... | collective-permute-start | bytes 3145736 | tf_op jit(solution)/shard_map/ppermute | solution.py:874
  37.5 20.1 %copy-start.1 = (bf16[2,577,1024]{2,0,1:T(2,128)(2,1)S(1)}, bf16[2,577,1024]{2,0,1:T(2,128)(2,1)}, u32[]{:S(2)}) copy-start(bf16[2,577,1024]{2,0,1:T(2,128)(2,1)} %param.27) | copy-start | bytes 7090180
  37.5 29.9 %collective-permute-start = (f32[592,512]{1,0:T(8,128)}, f32[592,512]{1,0:T(8,128)}, u32[]{:S(2)}, u32[]{:S(2)}) collective-permute-start(f32[592,512]{1,0:T(8,128)} %get-tuple-element.59), channel_id=1, source_target_pairs={{0,1},{1,0},{2,3},{3,2},{4,5},{5,4},{6,7},{7,6},{8,9},{9,8},{10,11... | collective-permute-start | bytes 3637256 | tf_op jit(solution)/shard_map/ppermute | solution.py:874
  37.6 22.7 %collective-permute-start.2 = (f32[256,1024]{1,0:T(8,128)}, f32[256,1024]{1,0:T(8,128)S(1)}, u32[]{:S(2)}, u32[]{:S(2)}) collective-permute-start(f32[256,1024]{1,0:T(8,128)} %collective-permute-done.1.near_ref), channel_id=1, source_target_pairs={{0,2},{2,0},{4,6},{6,4},{8,10},{10,8},{12,14},{14,12},{16,18},{18,... | collective-permute-start | bytes 3145736 | tf_op jit(solution)/shard_map/ppermute | solution.py:911
  55.8 37.2 %collective-permute-start.4 = (f32[592,512]{1,0:T(8,128)}, f32[592,512]{1,0:T(8,128)}, u32[]{:S(2)}, u32[]{:S(2)}) collective-permute-start(f32[592,512]{1,0:T(8,128)} %get-tuple-element.63), channel_id=1, source_target_pairs={{0,1},{1,0},{2,3},{3,2},{4,5},{5,4},{6,7},{7,6},{8,9},{9,8},{10,11... | collective-permute-start | bytes 3637256 | tf_op jit(solution)/shard_map/ppermute | solution.py:874
  60.4 1.0 copy-start.2
  90.6 450.0 %collective-permute-start.3 = (f32[592,1024]{1,0:T(8,128)}, f32[592,1024]{1,0:T(8,128)}, u32[]{:S(2)}, u32[]{:S(2)}) collective-permute-start(f32[592,1024]{1,0:T(8,128)} %get-tuple-element.61.own_ref), channel_id=1, source_target_pairs={{0,1},{1,0},{2,3},{3,2},{4,5},{5,4},{6,7},{7,6},{8,9},{9,8},{10,11... | collective-permute-start | bytes 7274504 | tf_op jit(solution)/shard_map/ppermute | solution.py:874
  90.7 266.3 %collective-permute-start.6 = (f32[592,1024]{1,0:T(8,128)}, f32[592,1024]{1,0:T(8,128)S(1)}, u32[]{:S(2)}, u32[]{:S(2)}) collective-permute-start(f32[592,1024]{1,0:T(8,128)} %get-tuple-element.66.refs_0_), channel_id=1, source_target_pairs={{0,1},{1,0},{2,3},{3,2},{4,5},{5,4},{6,7},{7,6},{8,9},{9,8},{10,11... | collective-permute-start | bytes 7274504 | tf_op jit(solution)/shard_map/ppermute | solution.py:874
  92.9 25.4 %copy-start.6 = (f32[1,2048]{1,0:T(1,128)S(1)}, f32[1,2048]{1,0:T(1,128)}, u32[]{:S(2)}) copy-start(f32[1,2048]{1,0:T(1,128)} %get-tuple-element.95) | copy-start | bytes 24580
  116.2 419.8 %collective-permute-start.5 = (f32[592,1024]{1,0:T(8,128)}, f32[592,1024]{1,0:T(8,128)}, u32[]{:S(2)}, u32[]{:S(2)}) collective-permute-start(f32[592,1024]{1,0:T(8,128)} %get-tuple-element.65.own_ref), channel_id=1, source_target_pairs={{0,1},{1,0},{2,3},{3,2},{4,5},{5,4},{6,7},{7,6},{8,9},{9,8},{10,11... | collective-permute-start | bytes 7274504 | tf_op jit(solution)/shard_map/ppermute | solution.py:874
  116.6 183.2 %collective-permute-start.8 = (f32[592,1024]{1,0:T(8,128)}, f32[592,1024]{1,0:T(8,128)}, u32[]{:S(2)}, u32[]{:S(2)}) collective-permute-start(f32[592,1024]{1,0:T(8,128)} %get-tuple-element.76.refs_0_), channel_id=1, source_target_pairs={{0,1},{1,0},{2,3},{3,2},{4,5},{5,4},{6,7},{7,6},{8,9},{9,8},{10,11... | collective-permute-start | bytes 7274504 | tf_op jit(solution)/shard_map/ppermute | solution.py:874
  357.0 1.4 copy-start.10
  358.4 57.5 %copy-start.7 = (f32[2,1024]{1,0:T(2,128)S(1)}, f32[2,1024]{1,0:T(2,128)}, u32[]{:S(2)}) copy-start(f32[2,1024]{1,0:T(2,128)} %get-tuple-element.98) | copy-start | bytes 24580
  358.4 58.2 %copy-start.5 = (f32[4,1024]{1,0:T(4,128)S(1)}, f32[4,1024]{1,0:T(4,128)}, u32[]{:S(2)}) copy-start(f32[4,1024]{1,0:T(4,128)} %get-tuple-element.96) | copy-start | bytes 49156
  358.4 59.0 %copy-start.9 = (f32[1,512]{1,0:T(1,128)S(1)}, f32[1,512]{1,0:T(1,128)}, u32[]{:S(2)}) copy-start(f32[1,512]{1,0:T(1,128)} %get-tuple-element.92) | copy-start | bytes 6148
  358.4 59.6 %copy-start.8 = (f32[1,512]{1,0:T(1,128)S(1)}, f32[1,512]{1,0:T(1,128)}, u32[]{:S(2)}) copy-start(f32[1,512]{1,0:T(1,128)} %get-tuple-element.90) | copy-start | bytes 6148
  358.4 60.2 %copy-start.3 = (f32[9216]{0:T(1024)S(1)}, f32[9216]{0:T(1024)}, u32[]{:S(2)}) copy-start(f32[9216]{0:T(1024)} %custom-call) | copy-start | bytes 110596
  358.4 60.3 %copy-start.4 = (f32[1,2048]{1,0:T(1,128)S(1)}, f32[1,2048]{1,0:T(1,128)}, u32[]{:S(2)}) copy-start(f32[1,2048]{1,0:T(1,128)} %add.31) | copy-start | bytes 24580
  419.7 148.3 %collective-permute-start.7 = (f32[592,1024]{1,0:T(8,128)}, f32[592,1024]{1,0:T(8,128)}, u32[]{:S(2)}, u32[]{:S(2)}) collective-permute-start(f32[592,1024]{1,0:T(8,128)} %get-tuple-element.75.own_ref), channel_id=1, source_target_pairs={{0,1},{1,0},{2,3},{3,2},{4,5},{5,4},{6,7},{7,6},{8,9},{9,8},{10,11... | collective-permute-start | bytes 7274504 | tf_op jit(solution)/shard_map/ppermute | solution.py:874
  420.3 141.7 %collective-permute-start.9 = (f32[592,1024]{1,0:T(8,128)}, f32[592,1024]{1,0:T(8,128)}, u32[]{:S(2)}, u32[]{:S(2)}) collective-permute-start(f32[592,1024]{1,0:T(8,128)} %get-tuple-element.83.own_ref), channel_id=1, source_target_pairs={{0,1},{1,0},{2,3},{3,2},{4,5},{5,4},{6,7},{7,6},{8,9},{9,8},{10,11... | collective-permute-start | bytes 7274504 | tf_op jit(solution)/shard_map/ppermute | solution.py:874
  526.4 34.9 %collective-permute-start.10 = (f32[2,1024]{1,0:T(2,128)S(1)}, f32[2,1024]{1,0:T(2,128)S(1)}, u32[]{:S(2)}, u32[]{:S(2)}) collective-permute-start(f32[2,1024]{1,0:T(2,128)S(1)} %pad_maximum_fusion.1), channel_id=1, source_target_pairs={{0,1},{1,0},{2,3},{3,2},{4,5},{5,4},{6,7},{7,6},{8,9},{9,8},{10,11... | collective-permute-start | bytes 24584 | tf_op jit(solution)/shard_map/ppermute | solution.py:874
  574.1 13.9 %slice-start = ((s8[8388608]{0:T(1024)(128)(4,1)}), s8[4194304]{0:T(1024)(128)(4,1)S(1)}, s32[]{:S(2)}) async-start(s8[8388608]{0:T(1024)(128)(4,1)} %bitcast.60), calls=%async_computation | async-start | bytes 8388608
  580.0 8.0 %slice-start.1 = ((s8[8388608]{0:T(1024)(128)(4,1)}), s8[4194304]{0:T(1024)(128)(4,1)S(1)}, s32[]{:S(2)}) async-start(s8[8388608]{0:T(1024)(128)(4,1)} %bitcast.60), calls=%async_computation.1 | async-start | bytes 8388608
